TPU v7x, 128 devices: a whole 4x4x4 slice. The times are simulated.
128 devices in a mesh: dp: 8 (over y_lo, x), tensor: 16 (over z, y_hi, core).
Axes of the slice: x: 4, y: 4 (y_hi: 2, y_lo: 2; y = y_hi * 2 + y_lo), z: 4, core: 2. Of those that a mesh axis runs over, the one named last changes fastest.
Arguments:
- tokens: bfloat16 [8192, 2048], P(('dp', 'tensor')), may hold values from -12 to 12
- targets: bfloat16 [8192, 2048], P(('dp', 'tensor')), may hold values from -6 to 6
- learner_gain: float32 [2048], replicated, may hold values from 0.1 to 1.9
- learner_gate: bfloat16 [2048, 8192], P(None, 'tensor'), may hold values from -0.125 to 0.125
- learner_up: bfloat16 [2048, 8192], P(None, 'tensor'), may hold values from -0.125 to 0.125
- learner_down: bfloat16 [8192, 2048], P('tensor'), may hold values from -0.0625 to 0.0625
- frozen_gain: float32 [2048], replicated, may hold values from 0.1 to 1.9
- frozen_gate: bfloat16 [2048, 8192], P(None, 'tensor'), may hold values from -0.125 to 0.125
- frozen_up: bfloat16 [2048, 8192], P(None, 'tensor'), may hold values from -0.125 to 0.125
- frozen_down: bfloat16 [8192, 2048], P('tensor'), may hold values from -0.0625 to 0.0625
Outputs:
- scores: float32 [8192], P(('dp', 'tensor'))
- grad_tokens: bfloat16 [8192, 2048], P(('dp', 'tensor'))
- grad_gain: float32 [2048], replicated
- grad_gate: float32 [2048, 8192], P('dp', 'tensor')
- grad_up: float32 [2048, 8192], P('dp', 'tensor')
- grad_down: float32 [8192, 2048], P('tensor', 'dp')
All inputs are finite; a program needn't handle non-finite values.
Results may differ from a plain program's by a relative error of at most 0.0096.
Values may be sent and summed in bfloat16 or wider, within the bound.
A program may use at most 128 MiB of HBM per device.

v0:
```python
import math

import jax
import jax.numpy as jnp
from jax import lax
from jax.sharding import PartitionSpec as P


def in_one_piece(arrays, axis, dim, along):
    both = jnp.concatenate(arrays, axis=along)
    out, at, gathered = (lax.all_gather(both, axis, axis=dim, tiled=True), 0, [])
    for a in arrays:
        gathered.append(lax.slice_in_dim(out, at, at + a.shape[along], axis=along))
        at += a.shape[along]
    return tuple(gathered)


def split_up(value, dim, size):
    shape = value.shape
    blocks = value.reshape(*shape[:dim], size, shape[dim] // size, *shape[dim + 1 :])
    return jnp.moveaxis(blocks, dim, 0)


def sum_at_owner(value, axis, dim):
    blocks = split_up(value, dim, lax.axis_size(axis))
    arrived = lax.all_to_all(blocks, axis, split_axis=0, concat_axis=0, tiled=True)
    return arrived.astype(jnp.float32).sum(axis=0)


def sent_together(arrays, axis, dim, along):
    widths = [a.shape[along] for a in arrays]
    both = jnp.concatenate(arrays, axis=along)
    out = sum_at_owner(both, axis, dim)
    return tuple(jnp.split(out, [sum(widths[:k]) for k in range(1, len(widths))], axis=along))


def project_up(normed, w_gate, w_up, w_down):
    gate_pre = jnp.dot(normed, w_gate, preferred_element_type=jnp.float32)
    up_pre = jnp.dot(normed, w_up, preferred_element_type=jnp.float32)
    hidden = (jax.nn.silu(gate_pre) * up_pre).astype(jnp.bfloat16)
    partial_out = jnp.dot(hidden, w_down, preferred_element_type=jnp.float32)
    return (gate_pre, up_pre, hidden, partial_out)


def local(
    tokens,
    targets,
    learner_gain,
    learner_gate,
    learner_up,
    learner_down,
    frozen_gain,
    frozen_gate,
    frozen_up,
    frozen_down,
):
    xfloat = tokens.astype(jnp.float32)
    inv_rms = lax.rsqrt(jnp.mean(xfloat * xfloat, axis=-1, keepdims=True) + 1e-05)
    normed = (xfloat * inv_rms * learner_gain).astype(jnp.bfloat16)
    frozen_normed = (xfloat * inv_rms * frozen_gain).astype(jnp.bfloat16)
    normed_all, frozen_all = in_one_piece((normed, frozen_normed), "tensor", 0, 1)
    gate_pre, up_pre, hidden, partial_learned = project_up(
        normed_all, learner_gate, learner_up, learner_down
    )
    frozen_partial = project_up(frozen_all, frozen_gate, frozen_up, frozen_down)[3]
    learned, frozen_out = sent_together(
        (partial_learned.astype(jnp.bfloat16), frozen_partial.astype(jnp.bfloat16)), "tensor", 0, 1
    )
    goal = targets.astype(jnp.float32)
    root = math.sqrt(tokens.shape[1])
    miss = learned - goal
    frozen_miss = frozen_out - goal
    learner_loss = 0.5 * jnp.sum(miss * miss, axis=-1) / root
    frozen_loss = 0.5 * jnp.sum(frozen_miss * frozen_miss, axis=-1) / root
    scores = learner_loss - frozen_loss
    weight = jax.nn.sigmoid(scores)
    out_grad = (weight[:, None] * miss / root).astype(jnp.bfloat16)
    grads_all = lax.all_gather(out_grad, "tensor", axis=0, tiled=True)
    hidden_grad = jnp.dot(grads_all, learner_down.T, preferred_element_type=jnp.float32)
    sigma = jax.nn.sigmoid(gate_pre)
    gate_grad = (hidden_grad * up_pre * sigma * (1.0 + gate_pre * (1.0 - sigma))).astype(
        jnp.bfloat16
    )
    up_grad = (hidden_grad * gate_pre * sigma).astype(jnp.bfloat16)
    partial_normed = jnp.dot(
        gate_grad, learner_gate.T, preferred_element_type=jnp.float32
    ) + jnp.dot(up_grad, learner_up.T, preferred_element_type=jnp.float32)
    normed_grad = sum_at_owner(partial_normed.astype(jnp.bfloat16), "tensor", 0)
    gain_term = jnp.sum(normed_grad * xfloat * inv_rms, axis=0)
    grad_gain = lax.psum(gain_term, ("dp", "tensor"))
    scaled = learner_gain * normed_grad
    cubed = inv_rms * inv_rms * inv_rms
    grad_tokens = (
        inv_rms * scaled - xfloat * cubed * jnp.mean(scaled * xfloat, axis=-1, keepdims=True)
    ).astype(jnp.bfloat16)
    gate_term = jnp.einsum("td,tf->df", normed_all, gate_grad, preferred_element_type=jnp.float32)
    up_term = jnp.einsum("td,tf->df", normed_all, up_grad, preferred_element_type=jnp.float32)
    down_term = jnp.einsum("td,tf->df", grads_all, hidden, preferred_element_type=jnp.float32)
    grad_gate, grad_up, down_shard = sent_together(
        (
            gate_term.astype(jnp.bfloat16),
            up_term.astype(jnp.bfloat16),
            down_term.astype(jnp.bfloat16),
        ),
        "dp",
        0,
        1,
    )
    grad_down = down_shard.T
    return (scores, grad_tokens, grad_gain, grad_gate, grad_up, grad_down)


def solution(mesh):
    placed = (
        P(("dp", "tensor"), None),
        P(("dp", "tensor"), None),
        P(),
        P(None, "tensor"),
        P(None, "tensor"),
        P("tensor", None),
        P(),
        P(None, "tensor"),
        P(None, "tensor"),
        P("tensor", None),
    )
    return jax.shard_map(
        local,
        mesh=mesh,
        in_specs=placed,
        out_specs=(
            P(("dp", "tensor")),
            P(("dp", "tensor"), None),
            P(),
            P("dp", "tensor"),
            P("dp", "tensor"),
            P("tensor", "dp"),
        ),
        check_vma=False,
    )
```

profile of v0, /device:TPU:1, one launch (start us, length us, event | category | flops | bytes accessed | tf_op | source)
XLA Modules:
  0.0 515.8 jit_solution(17087560783303499383)
XLA Ops:
  7.2 0.0 copy-start
  7.2 0.0 all-gather.3.cloned.1.call-start
  7.2 1.2 fusion.21
  8.5 1.1 fusion.17
  9.6 0.8 pad_maximum_fusion.2
  10.5 0.0 all-gather.3.cloned.1.call-update
  10.5 0.0 all-gather.5.cloned.1.call-start
  10.5 77.0 %all-gather.3.cloned.1.call-done = bf16[1024,4096]{1,0:T(8,128)(2,1)} async-done(((bf16[64,4096]{1,0:T(8,128)(2,1)}), bf16[1024,4096]{1,0:T(8,128)(2,1)}) %all-gather.3.cloned.1.call-update) | async-done | bytes 8388624 | tf_op jit(solution)/shard_map/all_gather | solution.py:11
  87.5 5.3 %fusion.8 = f32[1024,512]{1,0:T(8,128)S(1)} fusion(bf16[2048,512]{1,0:T(8,128)(2,1)} %param.13, bf16[1024,4096]{1,0:T(8,128)(2,1)} %all-gather.3.cloned.1.call-done), kind=kOutput, calls=%fused_computation.20 | convolution fusion | flops 2147483648 | bytes 8388608 | tf_op jit(solution)/shard_map/dot_general | solution.py:38
  92.9 0.5 copy-done.8
  93.4 3.8 multiply_convert_fusion.3
  97.2 0.0 copy-done.13
  97.2 4.3 convolution_convert_fusion.1
  101.5 3.7 fusion.2
  105.2 10.6 %convolution_convert_fusion = bf16[1024,2048]{1,0:T(8,128)(2,1)} fusion(bf16[512,2048]{1,0:T(8,128)(2,1)} %param.19, f32[1024,512]{1,0:T(8,128)} %fusion.2, bf16[2048,512]{1,0:T(8,128)(2,1)} %param.18, bf16[1024,4096]{1,0:T(8,128)(2,1)} %all-gather.3.cloned.1.call-done), kind=kOutput, calls=%fused_computation.7 | convolution fusion | flops 4300210176 | bytes 14680064 | tf_op jit(solution)/shard_map/dot_general | solution.py:41
  115.8 7.8 %pad_maximum_fusion = bf16[1024,4096]{1,0:T(8,128)(2,1)} fusion(bf16[1024,2048]{1,0:T(8,128)(2,1)} %convolution_convert_fusion, bf16[1024,2048]{1,0:T(8,128)(2,1)} %convolution_convert_fusion.1), kind=kLoop, calls=%fused_computation.2 | loop fusion | flops 16777216 | bytes 16777216 | tf_op jit(solution)/shard_map/concatenate | solution.py:32
  123.6 99.4 %all_to_all.15 = bf16[16,64,4096]{2,1,0:T(8,128)(2,1)S(1)} all-to-all(bf16[16,64,4096]{2,1,0:T(8,128)(2,1)} %bitcast.25), channel_id=1, replica_groups=mesh['dp'=8,'tensor'=16] {'tensor'}, dimensions={0} | all-to-all | bytes 16777216 | tf_op jit(solution)/shard_map/all_to_all | solution.py:26
  223.0 1.6 convert_reduce_fusion
  224.6 0.2 multiply_reduce_fusion
  224.8 0.5 add_divide_fusion.1
  225.3 0.8 multiply_convert_fusion.4
  226.1 0.0 all-gather.5.cloned.1.call-update
  226.2 52.8 %all-gather.5.cloned.1.call-done = bf16[1024,2048]{1,0:T(8,128)(2,1)} async-done(((bf16[64,2048]{1,0:T(8,128)(2,1)}), bf16[1024,2048]{1,0:T(8,128)(2,1)}) %all-gather.5.cloned.1.call-update) | async-done | bytes 4194320 | tf_op jit(solution)/shard_map/all_gather | solution.py:78
  279.0 6.5 %multiply_convert_fusion = (bf16[1024,512]{1,0:T(8,128)(2,1)S(1)}, bf16[1024,512]{1,0:T(8,128)(2,1)S(1)}) fusion(f32[1024,512]{1,0:T(8,128)} %copy-done.13, f32[1024,512]{1,0:T(8,128)} %get-tuple-element.34, bf16[1024,2048]{1,0:T(8,128)(2,1)} %all-gather.5.cloned.1.call-done, bf16[512,2048]{1,0:T(8,128)(2,1)S(1)} %copy-done), kind=kOutput, calls=%fused_computation.22 | convolution fusion | flops 2154299392 | bytes 12582912 | tf_op jit(solution)/shard_map/dot_general | solution.py:79
  285.5 0.0 copy-start.9
  285.6 2.4 fusion.29
  288.0 4.3 add_convert_fusion
  292.3 4.7 all-to-all-start.1
  296.9 0.0 slice-start
  297.0 5.0 convolution_convert_fusion.2
  302.0 0.0 slice-start.1
  302.0 4.7 convolution_convert_fusion.3
  306.8 2.4 convolution_convert_fusion.4
  309.2 9.6 %pad_maximum_fusion.1 = bf16[2048,1536]{0,1:T(8,128)(2,1)S(1)} fusion(bf16[2048,512]{0,1:T(8,128)(2,1)S(1)} %convolution_convert_fusion.2, bf16[2048,512]{0,1:T(8,128)(2,1)S(1)} %convolution_convert_fusion.3, bf16[2048,512]{0,1:T(8,128)(2,1)S(1)} %convolution_convert_fusion.4), kind=kLoop, calls=%fused_computation.6 | loop fusion | flops 18874368 | bytes 12582912 | tf_op jit(solution)/shard_map/concatenate | solution.py:32
  318.8 3.1 copy.23
  321.9 25.9 %all-to-all-done.1 = bf16[16,64,2048]{2,1,0:T(8,128)(2,1)} async-done(((bf16[16,64,2048]{2,1,0:T(8,128)(2,1)}), bf16[16,64,2048]{2,1,0:T(8,128)(2,1)}, u32[]{:S(2)}, u32[]{:S(2)}) %all-to-all-start.1) | async-done | bytes 4194336 | tf_op jit(solution)/shard_map/all_to_all | solution.py:26
  347.8 5.0 all-to-all-start.2
  352.8 0.0 copy-start.2
  352.8 0.0 copy-start.4
  352.9 3.0 convert_reduce_fusion.2
  355.9 0.2 fusion.27
  356.1 145.1 %psum.7 = f32[2048]{0:T(1024)} all-reduce(f32[2048]{0:T(1024)S(1)} %get-tuple-element.20), channel_id=1, replica_groups=mesh['dp'=8,'tensor'=16] {'dp','tensor'}, use_global_device_ids=true, to_apply=%region_7.8 | all-reduce | flops 2048 | bytes 16384 | tf_op jit(solution)/shard_map/psum | solution.py:90
  501.2 0.9 fusion.24
  502.2 0.0 all-to-all-done.2
  502.2 3.9 convert_reduce_fusion.1
  506.1 0.9 slice_bitcast_fusion
  507.0 1.0 copy.20
  508.0 1.0 copy.19
  (27 shorter events, 0.1 us)
Async XLA Ops:
  7.2 90.0 %copy-start = (bf16[512,2048]{1,0:T(8,128)(2,1)S(1)}, bf16[512,2048]{1,0:T(8,128)(2,1)}, u32[]{:S(2)}) copy-start(bf16[512,2048]{1,0:T(8,128)(2,1)} %param.15) | copy-start | bytes 6291460
  7.2 80.3 %all-gather.3.cloned.1.call-start = ((), (), s32[]{:S(2)}) async-start(), calls=%async_computation.3 | async-start | bytes 8912896 | tf_op jit(solution)/shard_map/all_gather | solution.py:11
  10.5 268.5 %all-gather.5.cloned.1.call-start = ((), (), s32[]{:S(2)}) async-start(), calls=%async_computation.4 | async-start | bytes 4456448 | tf_op jit(solution)/shard_map/all_gather | solution.py:78
  87.5 5.3 %copy-start.5 = (bf16[1024,4096]{1,0:T(8,128)(2,1)S(1)}, bf16[1024,4096]{1,0:T(8,128)(2,1)}, u32[]{:S(2)}) copy-start(bf16[1024,4096]{1,0:T(8,128)(2,1)} %all-gather.3.cloned.1.call-done) | copy-start | bytes 25165828
  87.5 5.8 %copy-start.8 = (bf16[2048,512]{1,0:T(8,128)(2,1)S(1)}, bf16[2048,512]{1,0:T(8,128)(2,1)}, u32[]{:S(2)}) copy-start(bf16[2048,512]{1,0:T(8,128)(2,1)} %param.14) | copy-start | bytes 6291460
  93.4 3.8 copy-start.13
  97.2 4.3 copy-start.12
  97.2 4.3 copy-start.6
  223.0 1.6 copy-start.3
  279.0 6.6 %copy-start.7 = (bf16[2048,512]{1,0:T(8,128)(2,1)S(1)}, bf16[2048,512]{1,0:T(8,128)(2,1)}, u32[]{:S(2)}) copy-start(bf16[2048,512]{1,0:T(8,128)(2,1)} %param.13) | copy-start | bytes 6291460
  285.5 2.4 copy-start.10
  285.5 2.4 copy-start.9
  292.3 55.5 %all-to-all-start.1 = ((bf16[16,64,2048]{2,1,0:T(8,128)(2,1)}), bf16[16,64,2048]{2,1,0:T(8,128)(2,1)}, u32[]{:S(2)}, u32[]{:S(2)}) async-start(bf16[16,64,2048]{2,1,0:T(8,128)(2,1)} %bitcast.28), calls=%async_computation.1 | async-start | bytes 8388608 | tf_op jit(solution)/shard_map/all_to_all | solution.py:26
  296.9 9.8 %slice-start = ((s8[8388608]{0:T(1024)(128)(4,1)}), s8[4194304]{0:T(1024)(128)(4,1)S(1)}, s32[]{:S(2)}) async-start(s8[8388608]{0:T(1024)(128)(4,1)} %bitcast.29), calls=%async_computation.5 | async-start | bytes 8388608
  302.0 4.8 slice-start.1
  302.0 4.8 copy-start.11
  347.8 154.3 %all-to-all-start.2 = ((bf16[8,256,1536]{1,2,0:T(8,128)(2,1)}), bf16[8,256,1536]{1,2,0:T(8,128)(2,1)}, u32[]{:S(2)}, u32[]{:S(2)}) async-start(bf16[8,256,1536]{1,2,0:T(8,128)(2,1)} %bitcast.26), calls=%async_computation.2 | async-start | bytes 12582912 | tf_op jit(solution)/shard_map/all_to_all | solution.py:26
  352.8 3.1 copy-start.2
  352.8 3.1 copy-start.4
  502.2 6.8 %copy-start.1 = (bf16[512,2048]{1,0:T(8,128)(2,1)S(1)}, bf16[512,2048]{1,0:T(8,128)(2,1)}, u32[]{:S(2)}) copy-start(bf16[512,2048]{1,0:T(8,128)(2,1)} %param.15) | copy-start | bytes 6291460
Sparse Core Ops, SparseCore 0:
  11.0 76.4 all-gather.2
  226.3 52.6 all-gather.4
where the time goes:
time: 516 us
  blocking collectives  245 us (47%)
  waiting for transfers between devices  156 us (30%)
  matrix products  53.1 us (10%)
  other arithmetic  31.9 us (6%)
  between operations  14.3 us (3%)
  starting transfers between devices  9.77 us (2%)
  local copies, waits for them, and re-layouts  6.52 us (1%)
    psum x1, blocking collectives, local(): grad_gain = lax.psum(gain_term, ('dp', 'tensor'))  145 us
    all_to_all x1, blocking collectives, sum_at_owner(): lax.all_to_all(blocks, axis, split_axis=0, concat_axis=0, tiled=True)  99.4 us
    all_gather x1, waiting for transfers between devices, in_one_piece(): lax.all_gather(both, axis, axis=dim, tiled=True)  77 us
    all_gather x1, waiting for transfers between devices, local(): grads_all = lax.all_gather(out_grad, 'tensor', axis=0, tiled=True)  52.8 us
    all_to_all x2, waiting for transfers between devices, sum_at_owner(): lax.all_to_all(blocks, axis, split_axis=0, concat_axis=0, tiled=True)  25.9 us
    concatenate x2, other arithmetic, sent_together(): both = jnp.concatenate(arrays, axis=along)  17.4 us
    dot_general x2, matrix products, project_up(): partial_out = jnp.dot(hidden, w_down, preferred_element_type=jnp.float32)  14.9 us
  transfers between devices with their start and end apart: 4, of which 3 were waited for; matrix products, arithmetic and copies ran while one was open for 6% of the time, Pallas kernels for 0%

commit v1 on v0

v1 whole, which is shorter than its diff:
```python
import functools
import math

import jax
import jax.numpy as jnp
from jax import lax
from jax.experimental import pallas as pl
from jax.experimental.pallas import tpu as pltpu
from jax.sharding import PartitionSpec as P

F32 = jnp.float32
BF16 = jnp.bfloat16
MESH = pl.DeviceIdType.MESH
VMEM_LIMIT = 66_000_000
ROWS = 16


class Wires:
    def __init__(self, send_sems, recv_sems):
        self.send_sems, self.recv_sems, self.sent = send_sems, recv_sems, []

    def send(self, src, dst, out, into, device):
        copy = pltpu.make_async_remote_copy(
            src_ref=src,
            dst_ref=dst,
            send_sem=self.send_sems.at[out],
            recv_sem=self.recv_sems.at[into],
            device_id=device,
            device_id_type=MESH,
        )
        copy.start()
        self.sent.append(copy)

    def got(self, ref, into, device):
        pltpu.make_async_remote_copy(
            src_ref=ref,
            dst_ref=ref,
            send_sem=self.send_sems.at[0],
            recv_sem=self.recv_sems.at[into],
            device_id=device,
            device_id_type=MESH,
        ).wait_recv()

    def drain(self):
        for copy in self.sent:
            copy.wait_send()


class Seat:
    def __init__(self):
        t = lax.axis_index("tensor")
        self.t = t
        self.z, self.y, self.c = t // 4, (t // 2) % 2, t % 2
        self.zp, self.zm, self.zf = (self.z + 1) % 4, (self.z + 3) % 4, (self.z + 2) % 4
        self.o, self.s = 1 - self.y, 1 - self.c

    def dev(self, z, y, c):
        return {"tensor": z * 4 + y * 2 + c}

    def pairs(self, i):
        yy = (self.y + i // 2) % 2
        a, b = (self.z + i % 2) % 4, (self.z + 3 - i % 2) % 4
        return a * 2 + yy, b * 2 + yy


def meet(devices):
    barrier = pltpu.get_barrier_semaphore()
    for device in devices:
        pl.semaphore_signal(barrier, inc=1, device_id=device, device_id_type=MESH)
    pl.semaphore_wait(barrier, len(devices))


class Gather:
    def __init__(self, seat, own, full, send_sems, recv_sems):
        self.s, self.own, self.full = seat, own, full
        self.w = Wires(send_sems, recv_sems)
        self.half = own.shape[0] // 2

    def blk(self, z, y, c, part=None):
        ref = self.full.at[z * 2 + y, c]
        return ref if part is None else ref.at[pl.ds(part * self.half, self.half)]

    def pass_on(self, z, y, out, into, device, part=None):
        b = self.blk(z, y, self.s.c, part)
        self.w.send(b, b, out, into, device)

    def got(self, z, y, c, into, part=None):
        s = self.s
        self.w.got(self.blk(z, y, c, part), into, s.dev(s.z, s.y, s.s))

    def start(self):
        s = self.s
        home = self.blk(s.z, s.y, s.c)
        self.w.send(self.own, home, 0, 0, s.dev(s.zp, s.y, s.c))
        self.w.send(self.own, home, 1, 1, s.dev(s.zm, s.y, s.c))
        self.w.send(self.own, home, 2, 2, s.dev(s.z, s.o, s.c))
        self.w.send(self.own, home, 3, 9, s.dev(s.z, s.y, s.s))
        self.full[s.z * 2 + s.y, s.c] = self.own[...]

    def step(self, i):
        s = self.s
        up, down, sib = s.dev(s.zp, s.y, s.c), s.dev(s.zm, s.y, s.c), s.dev(s.z, s.y, s.s)
        if i == 0:
            self.got(s.zm, s.y, s.c, 0)
            self.pass_on(s.zm, s.y, 4, 5, up, 0)
            self.pass_on(s.zm, s.y, 6, 10, sib)
            self.got(s.zp, s.y, s.c, 1)
            self.pass_on(s.zp, s.y, 5, 6, down, 1)
            self.pass_on(s.zp, s.y, 7, 11, sib)
            self.got(s.z, s.y, s.s, 9)
            self.got(s.zm, s.y, s.s, 10)
        if i == 1:
            self.got(s.z, s.o, s.c, 2)
            self.pass_on(s.z, s.o, 8, 3, up)
            self.pass_on(s.z, s.o, 9, 4, down)
            self.pass_on(s.z, s.o, 10, 12, sib)
            self.got(s.zf, s.y, s.c, 5, 0)
            self.got(s.zf, s.y, s.c, 6, 1)
            self.pass_on(s.zf, s.y, 15, 15, sib)
            self.got(s.zp, s.y, s.s, 11)
            self.got(s.zf, s.y, s.s, 15)
        if i == 2:
            self.got(s.zm, s.o, s.c, 3)
            self.pass_on(s.zm, s.o, 11, 7, up, 0)
            self.pass_on(s.zm, s.o, 13, 13, sib)
            self.got(s.zp, s.o, s.c, 4)
            self.pass_on(s.zp, s.o, 12, 8, down, 1)
            self.pass_on(s.zp, s.o, 14, 14, sib)
            self.got(s.z, s.o, s.s, 12)
            self.got(s.zm, s.o, s.s, 13)
        if i == 3:
            self.got(s.zf, s.o, s.c, 7, 0)
            self.got(s.zf, s.o, s.c, 8, 1)
            self.pass_on(s.zf, s.o, 16, 16, sib)
            self.got(s.zp, s.o, s.s, 14)
            self.got(s.zf, s.o, s.s, 16)


def fold(dst, refs, lo=0, hi=None):
    hi = dst.shape[0] if hi is None else hi

    def rows(k, carry):
        at = pl.ds(pl.multiple_of(lo + k * ROWS, ROWS), ROWS)
        total = refs[0][at].astype(F32)
        for ref in refs[1:]:
            total = total + ref[at].astype(F32)
        dst[at] = total.astype(dst.dtype)
        return carry

    lax.fori_loop(0, (hi - lo) // ROWS, rows, 0)


class RingSum:
    def __init__(self, block, dev, ring, row, slots, last, send_sems, recv_sems, base):
        self.block, self.dev, self.slots, self.last, self.base = block, dev, slots, last, base
        self.r, self.y, self.o = ring, row, 1 - row
        self.rp, self.rm, self.rf = (ring + 1) % 4, (ring + 3) % 4, (ring + 2) % 4
        self.w = Wires(send_sems, recv_sems)

    def out(self, r, y, slot, to, more=()):
        refs = self.block(r, y)
        if len(refs) + len(more) > 1:
            fold(refs[0], refs + [self.slots.at[k] for k in more])
        self.w.send(refs[0], self.slots.at[slot], self.base + slot, self.base + slot, to)

    def got(self, slot):
        self.w.got(self.slots.at[slot], self.base + slot, self.dev(self.rp, self.y))

    def stage1(self):
        up, down = self.dev(self.rp, self.y), self.dev(self.rm, self.y)
        self.out(self.rf, 0, 0, up)
        self.out(self.rf, 1, 1, down)
        self.out(self.rp, 1, 3, up)
        self.out(self.rm, 0, 4, down)

    def stage2(self):
        self.got(0)
        self.out(self.rp, 0, 2, self.dev(self.rp, self.y), (0,))
        self.got(1)
        self.out(self.rm, 1, 5, self.dev(self.rm, self.y), (1,))

    def stage3(self):
        for k in (3, 4, 2, 5):
            self.got(k)
        refs = self.block(self.r, self.o)
        fold(refs[0], refs + [self.slots.at[2 + self.o], self.slots.at[4 + self.o]])
        self.w.send(refs[0], self.last, self.base + 6, self.base + 6, self.dev(self.r, self.o))

    def stage4(self):
        self.w.got(self.last, self.base + 6, self.dev(self.r, self.o))
        refs = self.block(self.r, self.y)
        return refs + [self.slots.at[2 + self.y], self.slots.at[4 + self.y], self.last]


class GroupSum(RingSum):
    def __init__(self, seat, partial, paired, slots, last, send_sems, recv_sems):
        self.s, self.partial, self.paired = seat, partial, paired
        super().__init__(
            lambda z, y: [partial.at[z * 2 + y, seat.c], paired.at[z * 2 + y]],
            lambda z, y: seat.dev(z, y, seat.c),
            seat.z,
            seat.y,
            slots,
            last,
            send_sems,
            recv_sems,
            8,
        )

    def pair_send(self, i):
        s = self.s
        for j, p in enumerate(s.pairs(i)):
            k = 2 * i + j
            self.w.send(self.partial.at[p, s.s], self.paired.at[p], k, k, s.dev(s.z, s.y, s.s))

    def pair_got(self):
        s = self.s
        for i in range(4):
            for j, p in enumerate(s.pairs(i)):
                self.w.got(self.paired.at[p], 2 * i + j, s.dev(s.z, s.y, s.s))


def total_of(refs, at):
    total = refs[0][at].astype(F32)
    for ref in refs[1:]:
        total = total + ref[at].astype(F32)
    return total


def sigmoid(v):
    return 1.0 / (1.0 + jnp.exp(-v))


def dot(a, b):
    return jnp.dot(a, b, preferred_element_type=F32)


def dot_t(a, b):
    return lax.dot_general(a, b, (((1,), (1,)), ((), ())), preferred_element_type=F32)


def tile(j, size):
    return pl.ds(pl.multiple_of(j * size, size), size)


def rows_of(ref, p1, p2):
    width = ref.shape[-1]
    return jnp.concatenate([ref[p1].reshape(-1, width), ref[p2].reshape(-1, width)], axis=0)


def forward_kernel(
    tokens, targets, lgain, fgain, wg, wu, wd, fg, fu, fd,
    scores, ograd, normed_out, gate_out, up_out, hid_out,
    full, normed, fnormed, gate, up, hid_t, hid, lpart, fpart,
    lpaired, fpaired, lslots, fslots, llast, flast,
    vwg, vwu, vwd, vfg, vfu, vfd,
    load_sems, gsend, grecv, lsend, lrecv, fsend, frecv,
):
    seat = Seat()
    s = seat
    width = tokens.shape[1]
    hidden = vwg.shape[1]
    block = tokens.shape[0]
    loads = [
        pltpu.make_async_copy(src, dst, load_sems.at[k])
        for k, (src, dst) in enumerate(
            ((fg, vfg), (fu, vfu), (fd, vfd), (wg, vwg), (wu, vwu), (wd, vwd))
        )
    ]
    for copy in loads:
        copy.start()
    meet([s.dev(s.z, s.y, s.s), s.dev(s.zp, s.y, s.c), s.dev(s.zm, s.y, s.c), s.dev(s.z, s.o, s.c)])
    gather = Gather(s, tokens, full, gsend, grecv)
    learner = GroupSum(s, lpart, lpaired, lslots, llast, lsend, lrecv)
    frozen = GroupSum(s, fpart, fpaired, fslots, flast, fsend, frecv)
    gather.start()

    def normalize(i):
        for j, p in enumerate(s.pairs(i)):
            for core in range(2):

                def rows(k, carry, p=p, core=core, j=j):
                    at = pl.ds(pl.multiple_of(k * ROWS, ROWS), ROWS)
                    x = full[p, core, at].astype(F32)
                    unit = x * lax.rsqrt(jnp.mean(x * x, axis=-1, keepdims=True) + 1e-05)
                    normed[p, core, at] = (unit * lgain[...]).astype(BF16)
                    fnormed[j, core, at] = (unit * fgain[...]).astype(BF16)
                    return carry

                lax.fori_loop(0, block // ROWS, rows, 0)

    def put(part, i, cols, value):
        p1, p2 = s.pairs(i)
        value = value.astype(BF16).reshape(2, 2, block, value.shape[-1])
        part[p1, :, :, cols] = value[0]
        part[p2, :, :, cols] = value[1]

    nt, wt = min(256, hidden), min(512, width)

    def run_frozen(i):
        def cols(j, carry):
            at = tile(j, nt)
            lhs = rows_of(fnormed, 0, 1)
            g, u = dot(lhs, vfg[:, at]), dot(lhs, vfu[:, at])
            hid[:, at] = (g * sigmoid(g) * u).astype(BF16)
            return carry

        lax.fori_loop(0, hidden // nt, cols, 0)

        def outs(j, carry):
            at = tile(j, wt)
            put(fpart, i, at, dot(hid[...], vfd[:, at]))
            return carry

        lax.fori_loop(0, width // wt, outs, 0)

    def run_learner(i, carry):
        p1, p2 = s.pairs(i)
        n = 2 * block

        def cols(j, carry):
            at = tile(j, nt)
            lhs = rows_of(normed, p1, p2)
            g, u = dot(lhs, vwg[:, at]), dot(lhs, vwu[:, at])
            gate[p1, :, at], gate[p2, :, at] = g[:n], g[n:]
            up[p1, :, at], up[p2, :, at] = u[:n], u[n:]
            h = g * sigmoid(g) * u
            hid[:, at] = h.astype(BF16)
            ht = h.T.astype(BF16)
            hid_t[at, tile(p1, n)] = ht[:, :n]
            hid_t[at, tile(p2, n)] = ht[:, n:]
            return carry

        lax.fori_loop(0, hidden // nt, cols, 0)

        def outs(j, carry):
            at = tile(j, wt)
            put(lpart, i, at, dot(hid[...], vwd[:, at]))
            return carry

        lax.fori_loop(0, width // wt, outs, 0)
        return carry

    for i in range(4):
        gather.step(i)
        normalize(i)
        if i == 0:
            for copy in loads[:3]:
                copy.wait()
        run_frozen(i)
        frozen.pair_send(i)
    stores = [pltpu.make_async_copy(normed, normed_out, load_sems.at[6])]
    stores[0].start()
    for copy in loads[3:]:
        copy.wait()
    frozen.pair_got()
    frozen.stage1()
    lax.fori_loop(0, 2, run_learner, 0)
    learner.pair_send(0)
    learner.pair_send(1)
    frozen.stage2()
    lax.fori_loop(2, 4, run_learner, 0)
    learner.pair_send(2)
    learner.pair_send(3)
    for k, (src, dst) in enumerate(((gate, gate_out), (up, up_out), (hid_t, hid_out))):
        stores.append(pltpu.make_async_copy(src, dst, load_sems.at[7 + k]))
        stores[-1].start()
    learner.pair_got()
    learner.stage1()
    frozen.stage3()
    learner.stage2()
    learner.stage3()
    frefs = frozen.stage4()
    lrefs = learner.stage4()
    root = math.sqrt(width)

    def rows(k, carry):
        at = pl.ds(pl.multiple_of(k * ROWS, ROWS), ROWS)
        goal = targets[at].astype(F32)
        fmiss = total_of(frefs, at) - goal
        frozen_loss = 0.5 * jnp.sum(fmiss * fmiss, axis=-1, keepdims=True) / root
        miss = total_of(lrefs, at) - goal
        learner_loss = 0.5 * jnp.sum(miss * miss, axis=-1, keepdims=True) / root
        score = learner_loss - frozen_loss
        scores[at] = score
        ograd[at] = (sigmoid(score) * miss / root).astype(BF16)
        return carry

    lax.fori_loop(0, block // ROWS, rows, 0)
    for copy in stores:
        copy.wait()
    for part in (gather, learner, frozen):
        part.w.drain()


def backward_kernel(
    own, tokens, lgain, wg, wu, wd, normed_in, gate_in, up_in, hid_in,
    grad_tokens, grad_gain, out_gate, out_up, out_down,
    full, normed, gate, up, hid_t, gg, ug, ggt, ugt, terms,
    part, paired, slots, last, gslots, glast, uslots, ulast, dslots, dfar, dlast,
    gain_acc, gain_t, gain_d, vwg, vwu, vwd,
    load_sems, ssend, srecv, nsend, nrecv, qsend, qrecv, dsend, drecv, tsend, trecv, psend, precv,
):
    seat = Seat()
    s = seat
    d = lax.axis_index("dp")
    x, yl = d % 4, d // 4
    xp, xm, xf = (x + 1) % 4, (x + 3) % 4, (x + 2) % 4
    block, width = tokens.shape
    hidden = vwg.shape[1]
    cut = width // 8
    loads = [
        pltpu.make_async_copy(src, dst, load_sems.at[k])
        for k, (src, dst) in enumerate(
            (
                (wd, vwd), (gate_in, gate), (up_in, up), (normed_in, normed),
                (hid_in, hid_t), (wg, vwg), (wu, vwu),
            )
        )
    ]
    for copy in loads:
        copy.start()
    meet(
        [{"tensor": (s.t + r) % 16} for r in range(1, 16)]
        + [{"dp": (d + r) % 8} for r in range(1, 8)]
    )
    gather = Gather(s, own, full, ssend, srecv)
    gather.start()
    summed = GroupSum(s, part, paired, slots, last, nsend, nrecv)
    gate_sum = RingSum(
        lambda xx, yy: [terms.at[0, yy * 4 + xx]], lambda xx, yy: {"dp": yy * 4 + xx},
        x, yl, gslots, glast, qsend, qrecv, 0,
    )
    up_sum = RingSum(
        lambda xx, yy: [terms.at[1, yy * 4 + xx]], lambda xx, yy: {"dp": yy * 4 + xx},
        x, yl, uslots, ulast, qsend, qrecv, 7,
    )
    down_w = Wires(dsend, drecv)
    n = 2 * block
    nt, wt = min(256, hidden), min(512, width)

    def back(i):
        p1, p2 = s.pairs(i)

        def cols(j, carry):
            at = tile(j, nt)
            hg = dot_t(rows_of(full, p1, p2), vwd[at, :])
            g = jnp.concatenate([gate[p1, :, at], gate[p2, :, at]], axis=0)
            u = jnp.concatenate([up[p1, :, at], up[p2, :, at]], axis=0)
            sigma = sigmoid(g)
            side = hg * sigma
            ggrad = side * u * (1.0 + g * (1.0 - sigma))
            ugrad = side * g
            for value, plain, flipped in ((ggrad, gg, ggt), (ugrad, ug, ugt)):
                low = value.astype(BF16)
                plain[p1, :, at], plain[p2, :, at] = low[:n], low[n:]
                turned = value.T.astype(BF16)
                flipped[at, tile(p1, n)] = turned[:, :n]
                flipped[at, tile(p2, n)] = turned[:, n:]
            return carry

        lax.fori_loop(0, hidden // nt, cols, 0)

    for i in range(4):
        gather.step(i)
        if i == 0:
            for copy in loads[:3]:
                copy.wait()
        back(i)
    for copy in loads[3:]:
        copy.wait()

    def term(q, lhs, rhs, dd):
        at = tile(dd, cut)
        terms[q, dd] = dot(lhs[...], rhs[:, :, :, at].reshape(16 * block, cut)).astype(BF16)

    def ring_terms(q, lhs, lo, hi):
        def one(k, code):
            term(q, lhs, normed, (k % 2) * 4 + (x + code % 4) % 4)
            return code // 4

        lax.fori_loop(lo, hi, one, jnp.int32(3450 // 4**lo))

    def down_terms(row):
        def one(k, carry):
            term(2, hid_t, full, row * 4 + k)
            return carry

        lax.fori_loop(0, 4, one, 0)

    def normed_part(i, carry):
        p1, p2 = s.pairs(i)

        def outs(j, carry):
            at = tile(j, wt)
            value = dot_t(rows_of(gg, p1, p2), vwg[at, :]) + dot_t(rows_of(ug, p1, p2), vwu[at, :])
            value = value.astype(BF16).reshape(2, 2, block, wt)
            part[p1, :, :, at] = value[0]
            part[p2, :, :, at] = value[1]
            return carry

        lax.fori_loop(0, width // wt, outs, 0)
        return carry

    ring_terms(0, ggt, 0, 4)
    gate_sum.stage1()
    down_terms(1 - yl)
    across = {"dp": (1 - yl) * 4 + x}
    to_up, to_down = {"dp": yl * 4 + xp}, {"dp": yl * 4 + xm}
    for k in range(4):
        down_w.send(terms.at[2, (1 - yl) * 4 + k], dslots.at[k], k, k, across)
    ring_terms(0, ggt, 4, 8)
    ring_terms(1, ugt, 0, 4)
    up_sum.stage1()
    ring_terms(1, ugt, 4, 8)
    gate_sum.stage2()
    down_terms(yl)
    lax.fori_loop(0, 2, normed_part, 0)
    summed.pair_send(0)
    summed.pair_send(1)
    lax.fori_loop(2, 4, normed_part, 0)
    summed.pair_send(2)
    summed.pair_send(3)
    summed.pair_got()
    summed.stage1()
    for k in range(4):
        down_w.got(dslots.at[k], k, across)
    half = hidden // 2

    def mine(xx):
        return terms.at[2, yl * 4 + xx]

    def piece(ref, h):
        return ref.at[pl.ds(h * half, half)]

    fold(mine(xf), [mine(xf), dslots.at[xf]])
    down_w.send(piece(mine(xf), 0), dfar.at[0], 4, 4, to_up)
    down_w.send(piece(mine(xf), 1), dfar.at[1], 5, 5, to_down)
    fold(mine(xp), [mine(xp), dslots.at[xp]])
    down_w.send(piece(mine(xp), 1), piece(dlast.at[0], 1), 6, 6, to_up)
    fold(mine(xm), [mine(xm), dslots.at[xm]])
    down_w.send(piece(mine(xm), 0), piece(dlast.at[1], 0), 7, 7, to_down)
    up_sum.stage2()
    summed.stage2()
    down_w.got(dfar.at[0], 4, to_up)
    fold(piece(mine(xp), 0), [piece(mine(xp), 0), dfar.at[0]])
    down_w.send(piece(mine(xp), 0), piece(dlast.at[0], 0), 8, 8, to_up)
    down_w.got(dfar.at[1], 5, to_up)
    fold(piece(mine(xm), 1), [piece(mine(xm), 1), dfar.at[1]])
    down_w.send(piece(mine(xm), 1), piece(dlast.at[1], 1), 9, 9, to_down)
    summed.stage3()
    gate_sum.stage3()
    nrefs = summed.stage4()
    gain_acc[...] = jnp.zeros_like(gain_acc)

    def rows(k, carry):
        at = pl.ds(pl.multiple_of(k * ROWS, ROWS), ROWS)
        v = tokens[at].astype(F32)
        inv = lax.rsqrt(jnp.mean(v * v, axis=-1, keepdims=True) + 1e-05)
        ng = total_of(nrefs, at)
        scaled = ng * lgain[...]
        mid = jnp.mean(scaled * v, axis=-1, keepdims=True)
        grad_tokens[at] = (inv * scaled - v * (inv * inv * inv * mid)).astype(BF16)
        term = ng * v * inv
        gain_acc[...] += term[:8] + term[8:]
        return carry

    lax.fori_loop(0, block // ROWS, rows, 0)
    gain_t[s.t] = jnp.sum(gain_acc[...], axis=0, keepdims=True)
    tw, pw = Wires(tsend, trecv), Wires(psend, precv)
    for r in range(1, 16):
        tw.send(gain_t.at[s.t], gain_t.at[s.t], r - 1, r - 1, {"tensor": (s.t + r) % 16})
    up_sum.stage3()

    def finish(out, refs):
        def rows(k, carry):
            at = pl.ds(pl.multiple_of(k * ROWS, ROWS), ROWS)
            out[at] = total_of(refs, at)
            return carry

        lax.fori_loop(0, hidden // ROWS, rows, 0)

    finish(out_gate, gate_sum.stage4())
    for r in range(1, 16):
        tw.got(gain_t.at[(s.t + 16 - r) % 16], r - 1, {"tensor": (s.t + 1) % 16})
    gain_d[d] = jnp.sum(gain_t[...], axis=0)
    for r in range(1, 8):
        pw.send(gain_d.at[d], gain_d.at[d], r - 1, r - 1, {"dp": (d + r) % 8})
    for h in (1, 0):
        for k in (0, 1):
            at = ((8, 7), (6, 9))[h][k]
            down_w.got(piece(dlast.at[k], h), at, to_up)
    finish(out_down, [mine(x), dslots.at[x], dlast.at[0], dlast.at[1]])
    finish(out_up, up_sum.stage4())
    for r in range(1, 8):
        pw.got(gain_d.at[(d + 8 - r) % 8], r - 1, {"dp": (d + 1) % 8})
    grad_gain[...] = jnp.sum(gain_d[...], axis=0)
    for wires in (gather.w, summed.w, gate_sum.w, up_sum.w, down_w, tw, pw):
        wires.drain()


def local(
    tokens, targets, learner_gain, learner_gate, learner_up, learner_down,
    frozen_gain, frozen_gate, frozen_up, frozen_down,
):
    block, width = tokens.shape
    hidden = learner_gate.shape[1]
    dma = pltpu.SemaphoreType.DMA
    here = pl.BlockSpec(memory_space=pltpu.VMEM)
    away = pl.BlockSpec(memory_space=pl.ANY)
    shape = jax.ShapeDtypeStruct
    params = functools.partial(
        pltpu.CompilerParams, has_side_effects=True, vmem_limit_bytes=VMEM_LIMIT
    )
    gain = learner_gain.reshape(1, width)
    group = 16 * block
    up_w, down_w = pltpu.VMEM((width, hidden), BF16), pltpu.VMEM((hidden, width), BF16)
    sums = [
        pltpu.VMEM((8, block, width), BF16),
        pltpu.VMEM((6, block, width), BF16),
        pltpu.VMEM((block, width), BF16),
    ]
    blocks = pltpu.VMEM((8, 2, block, width), BF16)
    pre = pltpu.VMEM((8, 2 * block, hidden), F32)
    scores, ograd, normed, gate, up, hid_t = pl.pallas_call(
        forward_kernel,
        out_shape=(
            shape((block, 1), F32),
            shape((block, width), BF16),
            shape((8, 2, block, width), BF16),
            shape((8, 2 * block, hidden), F32),
            shape((8, 2 * block, hidden), F32),
            shape((hidden, group), BF16),
        ),
        in_specs=[here] * 4 + [away] * 6,
        out_specs=[here] * 2 + [away] * 4,
        scratch_shapes=[
            blocks,
            blocks,
            pltpu.VMEM((2, 2, block, width), BF16),
            pre,
            pre,
            pltpu.VMEM((hidden, group), BF16),
            pltpu.VMEM((4 * block, hidden), BF16),
            blocks,
            blocks,
            sums[0],
            sums[0],
            sums[1],
            sums[1],
            sums[2],
            sums[2],
            up_w,
            up_w,
            down_w,
            up_w,
            up_w,
            down_w,
            dma((10,)),
            dma((17,)),
            dma((17,)),
            dma((15,)),
            dma((15,)),
            dma((15,)),
            dma((15,)),
        ],
        compiler_params=params(collective_id=1),
        name="forward",
    )(
        tokens, targets, gain, frozen_gain.reshape(1, width), learner_gate, learner_up,
        learner_down, frozen_gate, frozen_up, frozen_down,
    )
    cut = width // 8
    mine = pltpu.VMEM((hidden, cut), BF16)
    grad = shape((hidden, cut), F32)
    flat = pltpu.VMEM((8, 2 * block, hidden), BF16)
    grad_tokens, grad_gain, grad_gate, grad_up, grad_down = pl.pallas_call(
        backward_kernel,
        out_shape=(shape((block, width), BF16), shape((1, width), F32), grad, grad, grad),
        in_specs=[here] * 3 + [away] * 7,
        out_specs=[here] * 5,
        scratch_shapes=[
            blocks,
            blocks,
            pre,
            pre,
            pltpu.VMEM((hidden, group), BF16),
            flat,
            flat,
            pltpu.VMEM((hidden, group), BF16),
            pltpu.VMEM((hidden, group), BF16),
            pltpu.VMEM((3, 8, hidden, cut), BF16),
            blocks,
            sums[0],
            sums[1],
            sums[2],
            pltpu.VMEM((6, hidden, cut), BF16),
            mine,
            pltpu.VMEM((6, hidden, cut), BF16),
            mine,
            pltpu.VMEM((4, hidden, cut), BF16),
            pltpu.VMEM((2, hidden // 2, cut), BF16),
            pltpu.VMEM((2, hidden, cut), BF16),
            pltpu.VMEM((8, width), F32),
            pltpu.VMEM((16, 1, width), F32),
            pltpu.VMEM((8, 1, width), F32),
            up_w,
            up_w,
            down_w,
            dma((7,)),
            dma((17,)),
            dma((17,)),
            dma((15,)),
            dma((15,)),
            dma((14,)),
            dma((14,)),
            dma((10,)),
            dma((10,)),
            dma((15,)),
            dma((15,)),
            dma((7,)),
            dma((7,)),
        ],
        compiler_params=params(collective_id=2),
        name="backward",
    )(ograd, tokens, gain, learner_gate, learner_up, learner_down, normed, gate, up, hid_t)
    return (
        scores.reshape(block),
        grad_tokens,
        grad_gain.reshape(width),
        grad_gate.T,
        grad_up.T,
        grad_down,
    )


def solution(mesh):
    placed = (
        P(("dp", "tensor"), None),
        P(("dp", "tensor"), None),
        P(),
        P(None, "tensor"),
        P(None, "tensor"),
        P("tensor", None),
        P(),
        P(None, "tensor"),
        P(None, "tensor"),
        P("tensor", None),
    )
    return jax.shard_map(
        local,
        mesh=mesh,
        in_specs=placed,
        out_specs=(
            P(("dp", "tensor")),
            P(("dp", "tensor"), None),
            P(),
            P("dp", "tensor"),
            P("dp", "tensor"),
            P("tensor", "dp"),
        ),
        check_vma=False,
    )
```

time: 516 us -> 193 us (0.37)
  blocking collectives: 245 us -> 0 us
  Pallas kernels: 0 us -> 184 us
  waiting for transfers between devices: 156 us -> 0 us
  matrix products: 53.1 us -> 0 us
  other arithmetic: 31.9 us -> 1.39 us
  between operations: 14.3 us -> 0.68 us
  starting transfers between devices: 9.77 us -> 0 us
    pallas_call x0 -> x2, Pallas kernels: none -> 184 us  [the longest x1 95.6 us: local(): pl.pallas_call(backward_kernel, out_shape=(shape((block, width), BF16), s...]
    psum x1 -> x0, blocking collectives: 145 us -> none  [local(): grad_gain = lax.psum(gain_term, ('dp', 'tensor'))]
    all_gather x2 -> x0, waiting for transfers between devices: 130 us -> none  [the longest x1 77 us: in_one_piece(): lax.all_gather(both, axis, axis=dim, tiled=True)]
    all_to_all x1 -> x0, blocking collectives: 99.4 us -> none  [sum_at_owner(): lax.all_to_all(blocks, axis, split_axis=0, concat_axis=0, tiled=True)]
    dot_general x11 -> x0, matrix products: 53.1 us -> none  [the longest x2 14.9 us: project_up(): partial_out = jnp.dot(hidden, w_down, preferred_element_type=jnp.float32)]
    all_to_all x2 -> x0, waiting for transfers between devices: 25.9 us -> none  [sum_at_owner(): lax.all_to_all(blocks, axis, split_axis=0, concat_axis=0, tiled=True)]
    concatenate x3 -> x0, other arithmetic: 18.3 us -> none  [the longest x2 17.4 us: sent_together(): both = jnp.concatenate(arrays, axis=along)]
    reduce_sum x6 -> x0, other arithmetic: 10.2 us -> none  [the longest x3 8.54 us: sum_at_owner(): return arrived.astype(jnp.float32).sum(axis=0)]
  transfers between devices with their start and end apart: 4 -> 0, of which waited for: 3 -> 0; matrix products, arithmetic and copies ran while one was open for 6% -> 0% of each run, Pallas kernels for 0% -> 0%
where the time goes in v1:
time: 193 us; the launch traced here: 192 us
  Pallas kernels  184 us (95%)
  local copies, waits for them, and re-layouts  6.25 us (3%)
    pallas_call x1, Pallas kernels, local(): pl.pallas_call(backward_kernel, out_shape=(shape((block, width), BF16), s...  95.6 us
    pallas_call x1, Pallas kernels, local(): pl.pallas_call(forward_kernel, out_shape=(shape((block, 1), F32), shape((...  88.5 us
    unnamed x11, local copies, waits for them, and re-layouts  6.25 us

profile of v1, /device:TPU:1, one launch (start us, length us, event | category | flops | bytes accessed | tf_op | source)
XLA Modules:
  0.0 192.4 jit_solution(5518374869678451726)
XLA Ops:
  0.6 88.5 %forward.1 = (f32[64,1]{1,0:T(8,128)}, bf16[64,2048]{1,0:T(8,128)(2,1)}, bf16[8,2,64,2048]{3,2,1,0:T(8,128)(2,1)}, f32[8,128,512]{2,1,0:T(8,128)}, f32[8,128,512]{2,1,0:T(8,128)}, /*index=5*/bf16[512,1024]{1,0:T(8,128)(2,1)}) custom-call(bf16[64,2048]{1,0:T(8,128)(2,1)} %tokens.3, bf16[64,2048]{1,0:T(8,128)(2,1)} %targets.1, f32[1,2048]{1,0:T(1,128)} %bitcast.7, ...), custom_call_target="tpu_custom_call" | custom-call | tf_op jit(solution)/shard_map/forward/pallas_call | solution.py:625
  89.2 1.4 reduce
  90.6 95.6 %backward.1 = (bf16[64,2048]{1,0:T(8,128)(2,1)}, f32[1,2048]{1,0:T(1,128)}, f32[512,256]{1,0:T(8,128)}, f32[512,256]{1,0:T(8,128)}, f32[512,256]{1,0:T(8,128)}) custom-call(bf16[64,2048]{1,0:T(8,128)(2,1)} %get-tuple-element.18.own, bf16[64,2048]{1,0:T(8,128)(2,1)} %tokens.3, f32[1,2048]{1,0:T(1,128)} %bitcast.8, bf16[2048,512]{1,0:T(8,128)(2,1)} %wg.3, ...), custom_call_target="tpu_custom_call" | custom-call | tf_op jit(solution)/shard_map/backward/pallas_call | solution.py:677
  186.1 0.0 copy-start.1
  186.1 0.0 copy-start.2
  186.2 0.0 copy-start
  186.2 2.1 %copy.18 = f32[256,512]{1,0:T(8,128)} copy(f32[256,512]{0,1:T(8,128)} %bitcast.6) | data formatting | bytes 1048576
  188.3 2.0 %copy.19 = f32[256,512]{1,0:T(8,128)} copy(f32[256,512]{0,1:T(8,128)} %bitcast.5) | data formatting | bytes 1048576
  190.3 0.0 copy-done.1
  190.3 0.7 copy.23
  191.0 0.0 copy-done.2
  191.0 0.6 copy.24
  191.6 0.0 copy-done
  191.6 0.8 copy.25
Async XLA Ops:
  186.1 4.2 %copy-start.1 = (bf16[64,2048]{1,0:T(8,128)(2,1)S(1)}, bf16[64,2048]{1,0:T(8,128)(2,1)}, u32[]{:S(2)}) copy-start(bf16[64,2048]{1,0:T(8,128)(2,1)} %get-tuple-element.47) | copy-start | bytes 786436
  186.1 4.9 %copy-start.2 = (f32[1,2048]{1,0:T(1,128)S(1)}, f32[1,2048]{1,0:T(1,128)}, u32[]{:S(2)}) copy-start(f32[1,2048]{1,0:T(1,128)} %get-tuple-element.24) | copy-start | bytes 24580
  186.2 5.5 %copy-start = (f32[512,256]{1,0:T(8,128)S(1)}, f32[512,256]{1,0:T(8,128)}, u32[]{:S(2)}) copy-start(f32[512,256]{1,0:T(8,128)} %get-tuple-element.51) | copy-start | bytes 1572868

commit v2 on v0

v2 whole, which is shorter than its diff:
```python
import functools
import math

import jax
import jax.numpy as jnp
from jax import lax
from jax.experimental import pallas as pl
from jax.experimental.pallas import tpu as pltpu
from jax.sharding import PartitionSpec as P

F32 = jnp.float32
BF16 = jnp.bfloat16
MESH = pl.DeviceIdType.MESH
VMEM_LIMIT = 66_000_000
ROWS = 16


def digits(*order):
    return sum(p * 8**k for k, p in enumerate(order))


ARRIVAL = digits(0, 3, 1, 4, 2, 7, 6, 5)
LATE = digits(6, 2, 5, 7, 1, 3, 4, 0)
TERMS = digits(2, 6, 5, 3, 1, 7, 0, 4)
DOWN = digits(2, 1, 3, 0, 6, 5, 7, 4)
ALL, A, B, A0, A1, B0, B1 = (0, 4), (0, 2), (2, 4), (0, 1), (1, 2), (2, 3), (3, 4)


class Wires:
    def __init__(self, send_sems, recv_sems):
        self.send_sems, self.recv_sems, self.sent = send_sems, recv_sems, []

    def send(self, src, dst, out, into, device):
        copy = pltpu.make_async_remote_copy(
            src_ref=src,
            dst_ref=dst,
            send_sem=self.send_sems.at[out],
            recv_sem=self.recv_sems.at[into],
            device_id=device,
            device_id_type=MESH,
        )
        copy.start()
        self.sent.append(copy)

    def got(self, ref, into, device):
        pltpu.make_async_remote_copy(
            src_ref=ref,
            dst_ref=ref,
            send_sem=self.send_sems.at[0],
            recv_sem=self.recv_sems.at[into],
            device_id=device,
            device_id_type=MESH,
        ).wait_recv()

    def drain(self):
        for copy in self.sent:
            copy.wait_send()


class Seat:
    def __init__(self):
        t = lax.axis_index("tensor")
        self.t = t
        self.z, self.y, self.c = t // 4, (t // 2) % 2, t % 2
        self.zp, self.zm, self.zf = (self.z + 1) % 4, (self.z + 3) % 4, (self.z + 2) % 4
        self.o, self.s = 1 - self.y, 1 - self.c

    def dev(self, z, y, c):
        return {"tensor": z * 4 + y * 2 + c}

    def pairs_of(self, code):
        first, second = code % 8, (code // 8) % 8
        return tuple(
            ((self.z + p % 4) % 4) * 2 + (self.y + p // 4) % 2 for p in (first, second)
        )

    def pairs(self, i, order):
        return self.pairs_of(order // 64**i)


def meet(devices):
    barrier = pltpu.get_barrier_semaphore()
    for device in devices:
        pl.semaphore_signal(barrier, inc=1, device_id=device, device_id_type=MESH)
    pl.semaphore_wait(barrier, len(devices))


class Gather:
    def __init__(self, seat, own, full, send_sems, recv_sems):
        self.s, self.own, self.full = seat, own, full
        self.w = Wires(send_sems, recv_sems)
        self.quarter = own.shape[0] // 4

    def rows(self, part):
        return pl.ds(part[0] * self.quarter, (part[1] - part[0]) * self.quarter)

    def blk(self, z, y, c, part):
        return self.full.at[z * 2 + y, c, self.rows(part)]

    def own_to(self, part, out, into, device):
        s = self.s
        self.w.send(self.own.at[self.rows(part)], self.blk(s.z, s.y, s.c, part), out, into, device)

    def pass_on(self, z, y, part, out, into, device):
        b = self.blk(z, y, self.s.c, part)
        self.w.send(b, b, out, into, device)

    def got(self, z, y, part, into):
        s = self.s
        self.w.got(self.blk(z, y, s.c, part), into, s.dev(s.z, s.y, s.s))

    def start(self):
        s = self.s
        up, down, across = s.dev(s.zp, s.y, s.c), s.dev(s.zm, s.y, s.c), s.dev(s.z, s.o, s.c)
        self.own_to(B, 0, 0, up)
        self.own_to(B, 1, 2, down)
        self.own_to(A, 2, 8, across)
        self.own_to(A, 3, 1, up)
        self.own_to(A, 4, 3, down)
        self.own_to(B, 5, 9, across)
        self.own_to(ALL, 6, 17, s.dev(s.z, s.y, s.s))
        self.full[s.z * 2 + s.y, s.c] = self.own[...]

    def arrive(self, *events):
        s = self.s
        z, zp, zm, zf, y, o = s.z, s.zp, s.zm, s.zf, s.y, s.o
        up, down, across = s.dev(zp, y, s.c), s.dev(zm, y, s.c), s.dev(z, o, s.c)
        sib = s.dev(z, y, s.s)
        for e in events:
            if e == 0:
                self.got(zm, y, B, 0)
                self.pass_on(zm, y, B0, 7, 4, up)
                self.pass_on(zm, y, B, 9, 11, across)
                self.got(zp, y, B, 2)
                self.pass_on(zp, y, B1, 8, 5, down)
                self.pass_on(zp, y, B, 10, 13, across)
            if e == 1:
                self.got(z, o, A, 8)
                self.pass_on(z, o, A, 12, 10, up)
                self.pass_on(z, o, A, 13, 12, down)
            if e == 2:
                self.got(zm, y, A, 1)
                self.pass_on(zm, y, A0, 14, 6, up)
                self.pass_on(zm, y, ALL, 18, 18, sib)
                self.got(zp, y, A, 3)
                self.pass_on(zp, y, A1, 15, 7, down)
                self.pass_on(zp, y, ALL, 19, 19, sib)
            if e == 3:
                self.got(z, o, B, 9)
                self.pass_on(z, o, ALL, 21, 21, sib)
            if e == 4:
                self.got(zf, y, B0, 4)
                self.got(zf, y, B1, 5)
                self.pass_on(zf, y, B, 11, 16, across)
            if e == 5:
                self.got(zm, o, A, 10)
                self.pass_on(zm, o, A0, 16, 14, up)
                self.got(zp, o, A, 12)
                self.pass_on(zp, o, A1, 17, 15, down)
            if e == 6:
                self.got(zf, y, A0, 6)
                self.got(zf, y, A1, 7)
                self.pass_on(zf, y, ALL, 20, 20, sib)
            if e == 7:
                self.got(zm, o, B, 11)
                self.pass_on(zm, o, ALL, 22, 22, sib)
                self.got(zp, o, B, 13)
                self.pass_on(zp, o, ALL, 23, 23, sib)
            if e == 8:
                self.got(zf, o, A0, 14)
                self.got(zf, o, A1, 15)
                self.got(zf, o, B, 16)
                self.pass_on(zf, o, ALL, 24, 24, sib)

    def have(self, i):
        s = self.s
        sib = s.dev(s.z, s.y, s.s)
        for p, k in zip(s.pairs(i, ARRIVAL), ((17, 18), (19, 21), (20, 22), (24, 23))[i]):
            self.w.got(self.full.at[p, s.s], k, sib)


def fold(dst, refs):
    def rows(k, carry):
        at = pl.ds(pl.multiple_of(k * ROWS, ROWS), ROWS)
        dst[at] = total_of(refs, at).astype(dst.dtype)
        return carry

    lax.fori_loop(0, dst.shape[0] // ROWS, rows, 0)


class RingFirst:
    def __init__(self, block, dev, ring, row, slots, last, send_sems, recv_sems, base):
        self.block, self.dev, self.slots, self.last, self.base = block, dev, slots, last, base
        self.r, self.y, self.o = ring, row, 1 - row
        self.rp, self.rm, self.rf = (ring + 1) % 4, (ring + 3) % 4, (ring + 2) % 4
        self.w = Wires(send_sems, recv_sems)

    def out(self, r, y, slot, to, more=()):
        refs = self.block(r, y)
        if len(refs) + len(more) > 1:
            fold(refs[0], refs + [self.slots.at[k] for k in more])
        self.w.send(refs[0], self.slots.at[slot], self.base + slot, self.base + slot, to)

    def got(self, slot):
        self.w.got(self.slots.at[slot], self.base + slot, self.dev(self.rp, self.y))

    def ready(self, off, rel):
        up, down = self.dev(self.rp, self.y), self.dev(self.rm, self.y)
        if (off, rel) == (2, 1):
            self.out(self.rf, self.o, 0, up)
        if (off, rel) == (2, 0):
            self.out(self.rf, self.y, 1, down)
        if (off, rel) == (1, 0):
            self.out(self.rp, self.y, 3, up)
        if (off, rel) == (3, 1):
            self.out(self.rm, self.o, 4, down)

    def stage2(self):
        self.got(0)
        self.out(self.rp, self.o, 2, self.dev(self.rp, self.y), (0,))
        self.got(1)
        self.out(self.rm, self.y, 5, self.dev(self.rm, self.y), (1,))

    def stage3(self):
        self.got(4)
        self.got(2)
        refs = self.block(self.r, self.o)
        fold(refs[0], refs + [self.slots.at[2], self.slots.at[4]])
        self.w.send(refs[0], self.last, self.base + 6, self.base + 6, self.dev(self.r, self.o))

    def stage4(self):
        self.got(3)
        self.got(5)
        self.w.got(self.last, self.base + 6, self.dev(self.r, self.o))
        return self.block(self.r, self.y) + [self.slots.at[3], self.slots.at[5], self.last]


class RowFirst:
    def __init__(self, block, dev, ring, row, across, far, near, send_sems, recv_sems, base):
        self.block, self.dev, self.base = block, dev, base
        self.across, self.far, self.near = across, far, near
        self.r, self.y, self.o = ring, row, 1 - row
        self.rp, self.rm, self.rf = (ring + 1) % 4, (ring + 3) % 4, (ring + 2) % 4
        self.up, self.down, self.over = dev(self.rp, row), dev(self.rm, row), dev(ring, self.o)
        self.half = near.shape[1] // 2
        self.w = Wires(send_sems, recv_sems)

    def piece(self, ref, h):
        return ref.at[pl.ds(h * self.half, self.half)]

    def send(self, src, dst, k, to):
        self.w.send(src, dst, self.base + k, self.base + k, to)

    def got(self, ref, k):
        self.w.got(ref, self.base + k, self.over)

    def ready(self, off, rel):
        if rel == 1:
            r = (self.r + off) % 4
            refs = self.block(r, self.o)
            if len(refs) > 1:
                fold(refs[0], refs)
            self.send(refs[0], self.across.at[r], off, self.over)

    def joined(self, r, k):
        self.got(self.across.at[r], k)
        refs = self.block(r, self.y)
        fold(refs[0], refs + [self.across.at[r]])
        return refs[0]

    def far_out(self):
        ref = self.joined(self.rf, 2)
        self.send(self.piece(ref, 0), self.far.at[0], 4, self.up)
        self.send(self.piece(ref, 1), self.far.at[1], 5, self.down)

    def near_out(self):
        ref = self.joined(self.rp, 1)
        self.send(self.piece(ref, 1), self.piece(self.near.at[0], 1), 6, self.up)
        ref = self.joined(self.rm, 3)
        self.send(self.piece(ref, 0), self.piece(self.near.at[1], 0), 7, self.down)

    def stage3(self):
        self.got(self.far.at[0], 4)
        ref = self.piece(self.block(self.rp, self.y)[0], 0)
        fold(ref, [ref, self.far.at[0]])
        self.send(ref, self.piece(self.near.at[0], 0), 8, self.up)
        self.got(self.far.at[1], 5)
        ref = self.piece(self.block(self.rm, self.y)[0], 1)
        fold(ref, [ref, self.far.at[1]])
        self.send(ref, self.piece(self.near.at[1], 1), 9, self.down)

    def stage4(self):
        self.got(self.across.at[self.r], 0)
        for k, h, at in ((0, 1, 6), (1, 0, 7), (0, 0, 8), (1, 1, 9)):
            self.got(self.piece(self.near.at[k], h), at)
        return self.block(self.r, self.y) + [self.across.at[self.r], self.near.at[0], self.near.at[1]]


class GroupSum:
    def __init__(self, seat, order, partial, paired, ring_a, row_a, ring_b, send_sems, recv_sems):
        self.s, self.order, self.partial, self.paired = seat, order, partial, paired
        self.w = Wires(send_sems, recv_sems)
        half = paired.shape[1] // 2

        def block(h):
            at = pl.ds(h * half, half)
            return lambda z, y: [partial.at[z * 2 + y, seat.c, at], paired.at[z * 2 + y, at]]

        def dev(z, y):
            return seat.dev(z, y, seat.c)

        form, buffers = (RowFirst, row_a) if ring_a is None else (RingFirst, ring_a)
        self.a = form(block(0), dev, seat.z, seat.y, *buffers, send_sems, recv_sems, 15)
        self.b = RingFirst(block(1), dev, seat.z, seat.y, *ring_b, send_sems, recv_sems, 8)

    def pair_send(self, i):
        s = self.s
        for j, p in enumerate(s.pairs(i, self.order)):
            k = 2 * i + j
            self.w.send(self.partial.at[p, s.s], self.paired.at[p], k, k, s.dev(s.z, s.y, s.s))

    def ready(self, i):
        s = self.s
        for j, p in enumerate(s.pairs(i, self.order)):
            self.w.got(self.paired.at[p], 2 * i + j, s.dev(s.z, s.y, s.s))
        for j in range(2):
            place = self.order // 8 ** (2 * i + j) % 8
            self.b.ready(place % 4, place // 4)
            self.a.ready(place % 4, place // 4)

    def drain(self):
        for w in (self.w, self.a.w, self.b.w):
            w.drain()


def total_of(refs, at):
    total = refs[0][at].astype(F32)
    for ref in refs[1:]:
        total = total + ref[at].astype(F32)
    return total


def sigmoid(v):
    return 1.0 / (1.0 + jnp.exp(-v))


def dot(a, b):
    return jnp.dot(a, b, preferred_element_type=F32)


def dot_t(a, b):
    return lax.dot_general(a, b, (((1,), (1,)), ((), ())), preferred_element_type=F32)


def tile(j, size):
    return pl.ds(pl.multiple_of(j * size, size), size)


def rows_of(ref, p1, p2, at=slice(None)):
    parts = [ref[p, ..., at] for p in (p1, p2)]
    return jnp.concatenate([v.reshape(-1, v.shape[-1]) for v in parts], axis=0)


def kernel(
    tokens, targets, lgain, fgain, wg, wu, wd, fg, fu, fd,
    scores, grad_tokens, grad_gain, out_gate, out_up, out_down,
    full, normed, fnormed, gate, up, hid_t, hid, lpart, fpart,
    lpaired, fpaired, lslots, fslots, llast, flast, lacross, facross, lfar, ffar, lnear, fnear,
    vwg, vwu, vwd, terms, ograd, flat_scores,
    gg, ug, ggt, ugt, gslots, glast, uslots, ulast, dslots, dfar, dlast, gain_acc, gain_t, gain_d,
    o_scores, o_tokens, o_gain, o_gate, o_up, o_down,
    load_sems, out_sems, gsend, grecv, lsend, lrecv, fsend, frecv,
    qsend, qrecv, dsend, drecv, tsend, trecv, psend, precv,
):
    seat = Seat()
    s = seat
    d = lax.axis_index("dp")
    x, yl = d % 4, d // 4
    block, width = tokens.shape
    hidden, cut = vwg.shape[1], terms.shape[3]
    deep, wide = width // hidden, hidden // cut
    n = 2 * block
    wt = 2 * cut
    moves = []
    for q, src in ((0, fg), (1, fu)):
        for j in range(wide):
            for k in range(deep):
                part = src.at[pl.ds(k * hidden, hidden), pl.ds(j * cut, cut)]
                moves.append((part, terms.at[q, j * deep + k], q))
    moves += [(fd.at[:, pl.ds(k * cut, cut)], terms.at[2, k], 2) for k in range(8)]
    moves += [(wg, vwg, 3), (wu, vwu, 4), (wd, vwd, 5)]

    def loaded(ref, k):
        pltpu.make_async_copy(ref, ref, load_sems.at[k]).wait()

    peers = [{"tensor": (s.t + r) % 16} for r in range(1, 16)]
    peers += [{"dp": (d + r) % 8} for r in range(1, 8)]
    meet(peers)
    gather = Gather(s, tokens, full, gsend, grecv)
    gather.start()
    for src, dst, k in moves:
        pltpu.make_async_copy(src, dst, load_sems.at[k]).start()
    ring_l, ring_f = (lslots, llast), (fslots, flast)
    row_l, row_f = (lacross, lfar, lnear), (facross, ffar, fnear)
    learner = GroupSum(s, LATE, lpart, lpaired, None, row_l, ring_l, lsend, lrecv)
    frozen = GroupSum(s, ARRIVAL, fpart, fpaired, None, row_f, ring_f, fsend, frecv)

    def unit(ref, at):
        v = ref[at].astype(F32)
        return v * lax.rsqrt(jnp.mean(v * v, axis=-1, keepdims=True) + 1e-05)

    def normalize(src, dst, gain):
        def rows(k, carry):
            for h in range(2):
                at = pl.ds(pl.multiple_of(k * 2 * ROWS + h * ROWS, ROWS), ROWS)
                dst[at] = (unit(src, at) * gain[...]).astype(BF16)
            return carry

        lax.fori_loop(0, block // (2 * ROWS), rows, 0)

    def frozen_units(i):
        for j, p in enumerate(s.pairs(i, ARRIVAL)):
            for core in range(2):
                normalize(full.at[p, core], fnormed.at[j, core], fgain)

    def put(part, p1, p2, cols, value):
        value = value.astype(BF16).reshape(2, 2, block, value.shape[-1])
        part[p1, :, :, cols] = value[0]
        part[p2, :, :, cols] = value[1]

    def frozen_hidden():
        def cols(j, carry):
            lhs = rows_of(fnormed, 0, 1)
            at = pl.ds(j * deep, deep)
            g = dot(lhs, terms[0, at].reshape(width, cut))
            u = dot(lhs, terms[1, at].reshape(width, cut))
            hid[:, tile(j, cut)] = (g * sigmoid(g) * u).astype(BF16)
            return carry

        lax.fori_loop(0, wide, cols, 0)

    def frozen_out(i):
        p1, p2 = s.pairs(i, ARRIVAL)

        def outs(j, carry):
            lhs = hid[...]
            value = jnp.concatenate([dot(lhs, terms[2, 2 * j + k]) for k in range(2)], axis=1)
            put(fpart, p1, p2, tile(j, wt), value)
            return carry

        lax.fori_loop(0, 4, outs, 0)

    def learner_units(i):
        for p in s.pairs(i, LATE):
            for core in range(2):
                normalize(full.at[p, core], normed.at[p, core], lgain)

    def learner_hidden(i):
        p1, p2 = s.pairs(i, LATE)

        def cols(j, carry):
            at = tile(j, cut)
            lhs = rows_of(normed, p1, p2)
            g, u = dot(lhs, vwg[:, at]), dot(lhs, vwu[:, at])
            gate[p1, :, at], gate[p2, :, at] = g[:n], g[n:]
            up[p1, :, at], up[p2, :, at] = u[:n], u[n:]
            h = g * sigmoid(g) * u
            hid[:, at] = h.astype(BF16)
            ht = h.T.astype(BF16)
            hid_t[at, tile(p1, n)] = ht[:, :n]
            hid_t[at, tile(p2, n)] = ht[:, n:]
            return carry

        lax.fori_loop(0, wide, cols, 0)

    def learner_out(i):
        p1, p2 = s.pairs(i, LATE)

        def outs(j, carry):
            at = tile(j, wt)
            put(lpart, p1, p2, at, dot(hid[...], vwd[:, at]))
            return carry

        lax.fori_loop(0, width // wt, outs, 0)
        learner.pair_send(i)

    arrivals = (((0, 1, 2), (3, 4), (5,)), ((), (6,), (7,)), ((8,), (), ()), ((), (), ()))
    for i in range(4):
        gather.arrive(*arrivals[i][0])
        gather.have(i)
        frozen_units(i)
        gather.arrive(*arrivals[i][1])
        if i == 0:
            for q in range(3):
                loaded(terms.at[q], q)
        if i > 0:
            frozen.ready(i - 1)
        frozen_hidden()
        gather.arrive(*arrivals[i][2])
        frozen_out(i)
        frozen.pair_send(i)
    learner_units(0)
    frozen.ready(3)
    gather.w.drain()
    for k, ref in ((3, vwg), (4, vwu), (5, vwd)):
        loaded(ref, k)
    learner_hidden(0)
    learner_out(0)
    learner_units(1)
    learner.ready(0)
    learner_hidden(1)
    frozen.b.stage2()
    frozen.a.far_out()
    learner_out(1)
    learner_units(2)
    frozen.a.near_out()
    learner.ready(1)
    learner_hidden(2)
    learner_out(2)
    learner_units(3)
    learner.ready(2)
    frozen.b.stage3()
    learner_hidden(3)
    frozen.a.stage3()
    learner.b.stage2()
    learner_out(3)
    learner.a.far_out()
    learner.a.near_out()
    learner.ready(3)
    learner.b.stage3()
    learner.a.stage3()
    root = math.sqrt(width)

    def losses(frefs, lrefs, base):
        def rows(k, carry):
            at = pl.ds(pl.multiple_of(k * ROWS, ROWS), ROWS)
            here = pl.ds(pl.multiple_of(base + k * ROWS, ROWS), ROWS)
            goal = targets[here].astype(F32)
            fmiss = total_of(frefs, at) - goal
            frozen_loss = 0.5 * jnp.sum(fmiss * fmiss, axis=-1, keepdims=True) / root
            miss = total_of(lrefs, at) - goal
            learner_loss = 0.5 * jnp.sum(miss * miss, axis=-1, keepdims=True) / root
            score = learner_loss - frozen_loss
            flat_scores[here] = jnp.broadcast_to(score, (ROWS, flat_scores.shape[1]))
            ograd[here] = (sigmoid(score) * miss / root).astype(BF16)
            return carry

        lax.fori_loop(0, block // 2 // ROWS, rows, 0)

    fa, fb = frozen.a.stage4(), frozen.b.stage4()
    la = learner.a.stage4()
    losses(fa, la, 0)
    losses(fb, learner.b.stage4(), block // 2)
    regather = Gather(s, ograd, full, gsend, grecv)
    regather.start()
    outs = []

    def emit(src, dst):
        outs.append(pltpu.make_async_copy(src, dst, out_sems.at[len(outs)]))
        outs[-1].start()

    o_scores[...] = flat_scores[...].T[:1]
    gain_acc[...] = jnp.zeros_like(gain_acc)
    frozen.drain()

    learner.drain()
    summed = GroupSum(s, LATE, fpart, fpaired, ring_l, None, ring_f, fsend, frecv)

    def dp_dev(xx, yy):
        return {"dp": yy * 4 + xx}

    def dp_block(q):
        return lambda xx, yy: [terms.at[q, yy * 4 + xx]]

    gate_sum = RingFirst(dp_block(0), dp_dev, x, yl, gslots, glast, qsend, qrecv, 0)
    up_sum = RingFirst(dp_block(1), dp_dev, x, yl, uslots, ulast, qsend, qrecv, 7)
    down_sum = RowFirst(dp_block(2), dp_dev, x, yl, dslots, dfar, dlast, dsend, drecv, 0)

    def back(i):
        p1, p2 = s.pairs(i, ARRIVAL)

        def cols(j, carry):
            at = tile(j, cut)
            hg = dot_t(rows_of(full, p1, p2), vwd[at, :])
            g, u = rows_of(gate, p1, p2, at), rows_of(up, p1, p2, at)
            sigma = sigmoid(g)
            side = hg * sigma
            ggrad = side * u * (1.0 + g * (1.0 - sigma))
            ugrad = side * g
            for value, plain, flipped in ((ggrad, gg, ggt), (ugrad, ug, ugt)):
                low = value.astype(BF16)
                plain[p1, :, at], plain[p2, :, at] = low[:n], low[n:]
                turned = value.T.astype(BF16)
                flipped[at, tile(p1, n)] = turned[:, :n]
                flipped[at, tile(p2, n)] = turned[:, n:]
            return carry

        lax.fori_loop(0, wide, cols, 0)

    for i, events in enumerate(((0, 1, 2, 3), (4, 5), (6, 7), (8,))):
        regather.arrive(*events)
        regather.have(i)
        back(i)

    def term(q, lhs, rhs, dd):
        at = tile(dd, cut)
        terms[q, dd] = dot(lhs[...], rhs[:, :, :, at].reshape(16 * block, cut)).astype(BF16)

    def some_terms(q, lhs, rhs, order, lo, hi):
        def one(k, code):
            row, ring = (yl + 1 + code % 8 // 4) % 2, (x + code % 4) % 4
            term(q, lhs, rhs, row * 4 + ring)
            return code // 8

        lax.fori_loop(lo, hi, one, jnp.int32(order // 8**lo))

    def normed_part(i):
        p1, p2 = s.pairs(i, LATE)

        def outs(j, carry):
            at = tile(j, wt)
            value = dot_t(rows_of(gg, p1, p2), vwg[at, :]) + dot_t(rows_of(ug, p1, p2), vwu[at, :])
            put(fpart, p1, p2, at, value)
            gains = value * rows_of(normed, p1, p2, at).astype(F32)
            gain_acc[:, at] += gains.reshape(-1, 8, wt).sum(axis=0)
            return carry

        lax.fori_loop(0, width // wt, outs, 0)
        summed.pair_send(i)

    def ring_start(q, lhs, ring):
        some_terms(q, lhs, normed, TERMS, 0, 2)
        ring.ready(2, 1)
        ring.ready(2, 0)
        some_terms(q, lhs, normed, TERMS, 2, 4)
        ring.ready(1, 0)
        ring.ready(3, 1)

    ring_start(0, ggt, gate_sum)
    some_terms(2, hid_t, full, DOWN, 0, 4)
    for off in (2, 1, 3, 0):
        down_sum.ready(off, 1)
    ring_start(1, ugt, up_sum)
    normed_part(0)
    normed_part(1)
    summed.ready(0)
    normed_part(2)
    summed.ready(1)
    normed_part(3)
    summed.ready(2)
    gain_t[s.t] = jnp.sum(gain_acc[...], axis=0, keepdims=True) / lgain[...]
    tw, pw = Wires(tsend, trecv), Wires(psend, precv)
    for r in range(1, 16):
        tw.send(gain_t.at[s.t], gain_t.at[s.t], r - 1, r - 1, {"tensor": (s.t + r) % 16})
    some_terms(0, ggt, normed, TERMS, 4, 8)
    gate_sum.stage2()
    summed.ready(3)
    summed.a.stage2()
    summed.b.stage2()
    some_terms(1, ugt, normed, TERMS, 4, 8)
    some_terms(2, hid_t, full, DOWN, 4, 8)
    up_sum.stage2()
    down_sum.far_out()
    down_sum.near_out()
    summed.a.stage3()
    summed.b.stage3()
    for r in range(1, 16):
        tw.got(gain_t.at[(s.t + 16 - r) % 16], r - 1, {"tensor": (s.t + 1) % 16})
    gain_d[d] = jnp.sum(gain_t[...], axis=0)
    for r in range(1, 8):
        pw.send(gain_d.at[d], gain_d.at[d], r - 1, r - 1, {"dp": (d + r) % 8})
    gate_sum.stage3()
    up_sum.stage3()
    down_sum.stage3()

    def token_grads(nrefs, base):
        def rows(k, carry):
            at = pl.ds(pl.multiple_of(k * ROWS, ROWS), ROWS)
            here = pl.ds(pl.multiple_of(base + k * ROWS, ROWS), ROWS)
            v = tokens[here].astype(F32)
            inv = lax.rsqrt(jnp.mean(v * v, axis=-1, keepdims=True) + 1e-05)
            scaled = total_of(nrefs, at) * lgain[...]
            mid = jnp.mean(scaled * v, axis=-1, keepdims=True)
            o_tokens[here] = (inv * scaled - v * (inv * inv * inv * mid)).astype(BF16)
            return carry

        lax.fori_loop(0, block // 2 // ROWS, rows, 0)

    token_grads(summed.a.stage4(), 0)
    token_grads(summed.b.stage4(), block // 2)
    emit(o_tokens, grad_tokens)
    for r in range(1, 8):
        pw.got(gain_d.at[(d + 8 - r) % 8], r - 1, {"dp": (d + 1) % 8})
    o_gain[...] = jnp.sum(gain_d[...], axis=0)
    emit(o_gain, grad_gain)
    emit(o_scores, scores)

    def finish_plain(out, refs):
        def rows(k, carry):
            at = pl.ds(pl.multiple_of(k * ROWS, ROWS), ROWS)
            out[at] = total_of(refs, at)
            return carry

        lax.fori_loop(0, hidden // ROWS, rows, 0)

    def finish_turned(out, refs):
        def rows(k, carry):
            at = tile(k, 128)
            out[:, at] = total_of(refs, at).T
            return carry

        lax.fori_loop(0, hidden // 128, rows, 0)

    finish_turned(o_gate, gate_sum.stage4())
    emit(o_gate, out_gate)
    finish_turned(o_up, up_sum.stage4())
    emit(o_up, out_up)
    finish_plain(o_down, down_sum.stage4())
    emit(o_down, out_down)
    for wires in (summed, regather.w, gate_sum.w, up_sum.w, down_sum.w, tw, pw):
        wires.drain()
    for copy in outs:
        copy.wait()


def hand_over(count, *refs):
    srcs, dsts, held, sems = refs[:count], refs[count : 2 * count], refs[2 * count : -1], refs[-1]
    ins = [pltpu.make_async_copy(a, b, sems.at[0, k]) for k, (a, b) in enumerate(zip(srcs, held))]
    outs = [pltpu.make_async_copy(a, b, sems.at[1, k]) for k, (a, b) in enumerate(zip(held, dsts))]
    for copy in ins:
        copy.start()
    for copy, then in zip(ins, outs):
        copy.wait()
        then.start()
    for copy in outs:
        copy.wait()


def local(
    tokens, targets, learner_gain, learner_gate, learner_up, learner_down,
    frozen_gain, frozen_gate, frozen_up, frozen_down,
):
    block, width = tokens.shape
    hidden = learner_gate.shape[1]
    cut, group, half = width // 8, 16 * block, block // 2
    here = pl.BlockSpec(memory_space=pltpu.VMEM)
    away = pl.BlockSpec(memory_space=pl.ANY)
    shape, vmem = jax.ShapeDtypeStruct, pltpu.VMEM

    def dma(*counts):
        return [pltpu.SemaphoreType.DMA((k,)) for k in counts]

    def twice(*shapes):
        return [vmem((*lead, width), BF16) for lead in shapes for _ in range(2)]

    blocks = vmem((8, 2, block, width), BF16)
    pre = vmem((8, 2 * block, hidden), F32)
    flat = vmem((8, 2 * block, hidden), BF16)
    turned = vmem((hidden, group), BF16)
    ring, mine = vmem((6, hidden, cut), BF16), vmem((hidden, cut), BF16)
    shapes = (
        shape((1, block), F32),
        shape((block, width), BF16),
        shape((1, width), F32),
        shape((cut, hidden), F32),
        shape((cut, hidden), F32),
        shape((hidden, cut), F32),
    )
    held = [vmem(a.shape, a.dtype) for a in shapes]
    results = pl.pallas_call(
        kernel,
        out_shape=shapes,
        in_specs=[here] * 4 + [away] * 6,
        out_specs=[away] * 6,
        scratch_shapes=[blocks, blocks, vmem((2, 2, block, width), BF16), pre, pre, turned]
        + [vmem((4 * block, hidden), BF16), blocks, blocks]
        + twice((8, block), (6, half), (half,), (4, half), (2, half // 2), (2, half))
        + [vmem((width, hidden), BF16)] * 2
        + [vmem((hidden, width), BF16), vmem((3, 8, hidden, cut), BF16)]
        + [vmem((block, width), BF16), vmem((block, 128), F32), flat, flat, turned, turned]
        + [ring, mine, ring, mine]
        + [vmem((k, hidden // h, cut), BF16) for k, h in ((4, 1), (2, 2), (2, 1))]
        + [vmem((8, width), F32), vmem((16, 1, width), F32), vmem((8, 1, width), F32)]
        + held
        + dma(6, 6, 25, 25, 25, 25, 25, 25, 14, 14, 10, 10, 15, 15, 7, 7),
        compiler_params=pltpu.CompilerParams(
            has_side_effects=True, vmem_limit_bytes=VMEM_LIMIT, collective_id=1
        ),
        name="step",
    )(
        tokens, targets, learner_gain.reshape(1, width), frozen_gain.reshape(1, width),
        learner_gate, learner_up, learner_down, frozen_gate, frozen_up, frozen_down,
    )
    scores, grad_tokens, grad_gain, grad_gate, grad_up, grad_down = pl.pallas_call(
        functools.partial(hand_over, len(shapes)),
        out_shape=shapes,
        in_specs=[away] * 6,
        out_specs=[away] * 6,
        scratch_shapes=held + [pltpu.SemaphoreType.DMA((2, 6))],
        name="hand_over",
    )(*results)
    return (
        scores.reshape(block),
        grad_tokens,
        grad_gain.reshape(width),
        grad_gate,
        grad_up,
        grad_down,
    )


def solution(mesh):
    placed = (
        P(("dp", "tensor"), None),
        P(("dp", "tensor"), None),
        P(),
        P(None, "tensor"),
        P(None, "tensor"),
        P("tensor", None),
        P(),
        P(None, "tensor"),
        P(None, "tensor"),
        P("tensor", None),
    )
    return jax.shard_map(
        local,
        mesh=mesh,
        in_specs=placed,
        out_specs=(
            P(("dp", "tensor")),
            P(("dp", "tensor"), None),
            P(),
            P("dp", "tensor"),
            P("dp", "tensor"),
            P("tensor", "dp"),
        ),
        check_vma=False,
    )
```

time: 516 us -> 140 us (0.27)
  blocking collectives: 245 us -> 0 us
  waiting for transfers between devices: 156 us -> 0 us
  Pallas kernels: 0 us -> 139 us
  matrix products: 53.1 us -> 0 us
  other arithmetic: 31.9 us -> 0 us
  between operations: 14.3 us -> 0.8 us
  starting transfers between devices: 9.77 us -> 0 us
  local copies, waits for them, and re-layouts: 6.52 us -> 0 us
    psum x1 -> x0, blocking collectives: 145 us -> none  [local(): grad_gain = lax.psum(gain_term, ('dp', 'tensor'))]
    pallas_call x0 -> x2, Pallas kernels: none -> 139 us  [the longest x1 137 us: local(): pl.pallas_call(kernel, out_shape=shapes, in_specs=[here] * 4 + [away] * 6...]
    all_gather x2 -> x0, waiting for transfers between devices: 130 us -> none  [the longest x1 77 us: in_one_piece(): lax.all_gather(both, axis, axis=dim, tiled=True)]
    all_to_all x1 -> x0, blocking collectives: 99.4 us -> none  [sum_at_owner(): lax.all_to_all(blocks, axis, split_axis=0, concat_axis=0, tiled=True)]
    dot_general x11 -> x0, matrix products: 53.1 us -> none  [the longest x2 14.9 us: project_up(): partial_out = jnp.dot(hidden, w_down, preferred_element_type=jnp.float32)]
    all_to_all x2 -> x0, waiting for transfers between devices: 25.9 us -> none  [sum_at_owner(): lax.all_to_all(blocks, axis, split_axis=0, concat_axis=0, tiled=True)]
    concatenate x3 -> x0, other arithmetic: 18.3 us -> none  [the longest x2 17.4 us: sent_together(): both = jnp.concatenate(arrays, axis=along)]
    reduce_sum x6 -> x0, other arithmetic: 10.2 us -> none  [the longest x3 8.54 us: sum_at_owner(): return arrived.astype(jnp.float32).sum(axis=0)]
  transfers between devices with their start and end apart: 4 -> 0, of which waited for: 3 -> 0; matrix products, arithmetic and copies ran while one was open for 6% -> 0% of each run, Pallas kernels for 0% -> 0%
where the time goes in v2:
time: 140 us
  Pallas kernels  139 us (99%)
    pallas_call x1, Pallas kernels, local(): pl.pallas_call(kernel, out_shape=shapes, in_specs=[here] * 4 + [away] * 6...  137 us

profile of v2, /device:TPU:1, one launch (start us, length us, event | category | flops | bytes accessed | tf_op | source)
XLA Modules:
  0.0 139.8 jit_solution(4225691942745862760)
XLA Ops:
  0.6 136.6 %step.1 = (f32[1,64]{1,0:T(1,128)}, bf16[64,2048]{1,0:T(8,128)(2,1)}, f32[1,2048]{1,0:T(1,128)}, f32[256,512]{1,0:T(8,128)}, f32[256,512]{1,0:T(8,128)}, /*index=5*/f32[512,256]{1,0:T(8,128)}) custom-call(bf16[64,2048]{1,0:T(8,128)(2,1)} %tokens.1, bf16[64,2048]{1,0:T(8,128)(2,1)} %targets.1, f32[1,2048]{1,0:T(1,128)} %bitcast.4, f32[1,2048]{1,0:T(1,128)} %bitcast.5, ...), custom_call_target="tpu_custom_call" | custom-call | tf_op jit(solution)/shard_map/step/pallas_call | solution.py:770
  137.2 2.4 %hand_over.1 = (f32[1,64]{1,0:T(1,128)}, bf16[64,2048]{1,0:T(8,128)(2,1)}, f32[1,2048]{1,0:T(1,128)}, f32[256,512]{1,0:T(8,128)}, f32[256,512]{1,0:T(8,128)}, /*index=5*/f32[512,256]{1,0:T(8,128)}) custom-call(f32[1,64]{1,0:T(1,128)} %get-tuple-element.18.refs_0_, bf16[64,2048]{1,0:T(8,128)(2,1)} %get-tuple-element.19.refs_1_, ...), custom_call_target="tpu_custom_call" | custom-call | tf_op jit(solution)/shard_map/hand_over/pallas_call | solution.py:794

commit v3 on v2

--- a/solution.py
+++ b/solution.py
@@ -20,7 +20,7 @@
 
 
 ARRIVAL = digits(0, 3, 1, 4, 2, 7, 6, 5)
-LATE = digits(6, 2, 5, 7, 1, 3, 4, 0)
+LATE = digits(6, 2, 5, 3, 7, 4, 1, 0)
 TERMS = digits(2, 6, 5, 3, 1, 7, 0, 4)
 DOWN = digits(2, 1, 3, 0, 6, 5, 7, 4)
 ALL, A, B, A0, A1, B0, B1 = (0, 4), (0, 2), (2, 4), (0, 1), (1, 2), (2, 3), (3, 4)
@@ -366,11 +366,12 @@
     scores, grad_tokens, grad_gain, out_gate, out_up, out_down,
     full, normed, fnormed, gate, up, hid_t, hid, lpart, fpart,
     lpaired, fpaired, lslots, fslots, llast, flast, lacross, facross, lfar, ffar, lnear, fnear,
+    again, nslots, nlast, turn_w, row_w, col_w,
     vwg, vwu, vwd, terms, ograd, flat_scores,
     gg, ug, ggt, ugt, gslots, glast, uslots, ulast, dslots, dfar, dlast, gain_acc, gain_t, gain_d,
     o_scores, o_tokens, o_gain, o_gate, o_up, o_down,
     load_sems, out_sems, gsend, grecv, lsend, lrecv, fsend, frecv,
-    qsend, qrecv, dsend, drecv, tsend, trecv, psend, precv,
+    qsend, qrecv, dsend, drecv, tsend, trecv, psend, precv, wsend, wrecv,
 ):
     seat = Seat()
     s = seat
@@ -381,14 +382,13 @@
     deep, wide = width // hidden, hidden // cut
     n = 2 * block
     wt = 2 * cut
-    moves = []
+    moves = [(wg, vwg, 3), (wu, vwu, 4), (wd, vwd, 5)]
     for q, src in ((0, fg), (1, fu)):
         for j in range(wide):
             for k in range(deep):
                 part = src.at[pl.ds(k * hidden, hidden), pl.ds(j * cut, cut)]
                 moves.append((part, terms.at[q, j * deep + k], q))
     moves += [(fd.at[:, pl.ds(k * cut, cut)], terms.at[2, k], 2) for k in range(8)]
-    moves += [(wg, vwg, 3), (wu, vwu, 4), (wd, vwd, 5)]
 
     def loaded(ref, k):
         pltpu.make_async_copy(ref, ref, load_sems.at[k]).wait()
@@ -402,26 +402,26 @@
         pltpu.make_async_copy(src, dst, load_sems.at[k]).start()
     ring_l, ring_f = (lslots, llast), (fslots, flast)
     row_l, row_f = (lacross, lfar, lnear), (facross, ffar, fnear)
-    learner = GroupSum(s, LATE, lpart, lpaired, None, row_l, ring_l, lsend, lrecv)
-    frozen = GroupSum(s, ARRIVAL, fpart, fpaired, None, row_f, ring_f, fsend, frecv)
+    learner = GroupSum(s, ARRIVAL, lpart, lpaired, None, row_l, ring_l, lsend, lrecv)
+    frozen = GroupSum(s, LATE, fpart, fpaired, None, row_f, ring_f, fsend, frecv)
 
     def unit(ref, at):
         v = ref[at].astype(F32)
         return v * lax.rsqrt(jnp.mean(v * v, axis=-1, keepdims=True) + 1e-05)
 
     def normalize(src, dst, gain):
-        def rows(k, carry):
-            for h in range(2):
-                at = pl.ds(pl.multiple_of(k * 2 * ROWS + h * ROWS, ROWS), ROWS)
-                dst[at] = (unit(src, at) * gain[...]).astype(BF16)
-            return carry
-
-        lax.fori_loop(0, block // (2 * ROWS), rows, 0)
+        for k in range(block // ROWS):
+            at = pl.ds(k * ROWS, ROWS)
+            dst[at] = (unit(src, at) * gain[...]).astype(BF16)
 
     def frozen_units(i):
-        for j, p in enumerate(s.pairs(i, ARRIVAL)):
-            for core in range(2):
+        for j, p in enumerate(s.pairs(i, LATE)):
+
+            def one(core, carry, j=j, p=p):
                 normalize(full.at[p, core], fnormed.at[j, core], fgain)
+                return carry
+
+            lax.fori_loop(0, 2, one, 0)
 
     def put(part, p1, p2, cols, value):
         value = value.astype(BF16).reshape(2, 2, block, value.shape[-1])
@@ -437,10 +437,10 @@
             hid[:, tile(j, cut)] = (g * sigmoid(g) * u).astype(BF16)
             return carry
 
-        lax.fori_loop(0, wide, cols, 0)
+        lax.fori_loop(0, wide, cols, 0, unroll=True)
 
     def frozen_out(i):
-        p1, p2 = s.pairs(i, ARRIVAL)
+        p1, p2 = s.pairs(i, LATE)
 
         def outs(j, carry):
             lhs = hid[...]
@@ -448,15 +448,20 @@
             put(fpart, p1, p2, tile(j, wt), value)
             return carry
 
-        lax.fori_loop(0, 4, outs, 0)
+        lax.fori_loop(0, 4, outs, 0, unroll=True)
+        frozen.pair_send(i)
 
     def learner_units(i):
-        for p in s.pairs(i, LATE):
-            for core in range(2):
+        for p in s.pairs(i, ARRIVAL):
+
+            def one(core, carry, p=p):
                 normalize(full.at[p, core], normed.at[p, core], lgain)
+                return carry
+
+            lax.fori_loop(0, 2, one, 0)
 
     def learner_hidden(i):
-        p1, p2 = s.pairs(i, LATE)
+        p1, p2 = s.pairs(i, ARRIVAL)
 
         def cols(j, carry):
             at = tile(j, cut)
@@ -471,100 +476,106 @@
             hid_t[at, tile(p2, n)] = ht[:, n:]
             return carry
 
-        lax.fori_loop(0, wide, cols, 0)
+        lax.fori_loop(0, wide, cols, 0, unroll=True)
 
     def learner_out(i):
-        p1, p2 = s.pairs(i, LATE)
+        p1, p2 = s.pairs(i, ARRIVAL)
 
         def outs(j, carry):
             at = tile(j, wt)
             put(lpart, p1, p2, at, dot(hid[...], vwd[:, at]))
             return carry
 
-        lax.fori_loop(0, width // wt, outs, 0)
+        lax.fori_loop(0, width // wt, outs, 0, unroll=True)
         learner.pair_send(i)
 
     arrivals = (((0, 1, 2), (3, 4), (5,)), ((), (6,), (7,)), ((8,), (), ()), ((), (), ()))
     for i in range(4):
         gather.arrive(*arrivals[i][0])
         gather.have(i)
-        frozen_units(i)
+        learner_units(i)
         gather.arrive(*arrivals[i][1])
         if i == 0:
-            for q in range(3):
-                loaded(terms.at[q], q)
+            for k, ref in ((3, vwg), (4, vwu), (5, vwd)):
+                loaded(ref, k)
         if i > 0:
-            frozen.ready(i - 1)
-        frozen_hidden()
+            learner.ready(i - 1)
+        learner_hidden(i)
         gather.arrive(*arrivals[i][2])
-        frozen_out(i)
-        frozen.pair_send(i)
-    learner_units(0)
-    frozen.ready(3)
+        learner_out(i)
+    frozen_units(0)
+    learner.ready(3)
     gather.w.drain()
-    for k, ref in ((3, vwg), (4, vwu), (5, vwd)):
-        loaded(ref, k)
-    learner_hidden(0)
-    learner_out(0)
-    learner_units(1)
-    learner.ready(0)
-    learner_hidden(1)
+    for q in range(3):
+        loaded(terms.at[q], q)
+    frozen_hidden()
+    frozen_out(0)
+    frozen_units(1)
+    frozen.ready(0)
+    frozen_hidden()
+    learner.b.stage2()
+    frozen_out(1)
+    frozen_units(2)
+    learner.a.far_out()
+    frozen.ready(1)
+    frozen_hidden()
+    learner.a.near_out()
+    frozen_out(2)
+    frozen_units(3)
+    learner.b.stage3()
+    frozen.ready(2)
+    learner.a.stage3()
     frozen.b.stage2()
+    frozen_hidden()
     frozen.a.far_out()
-    learner_out(1)
-    learner_units(2)
-    frozen.a.near_out()
-    learner.ready(1)
-    learner_hidden(2)
-    learner_out(2)
-    learner_units(3)
-    learner.ready(2)
-    frozen.b.stage3()
-    learner_hidden(3)
-    frozen.a.stage3()
-    learner.b.stage2()
-    learner_out(3)
-    learner.a.far_out()
-    learner.a.near_out()
-    learner.ready(3)
-    learner.b.stage3()
-    learner.a.stage3()
+    frozen_out(3)
     root = math.sqrt(width)
 
-    def losses(frefs, lrefs, base):
+    def misses(refs, base):
         def rows(k, carry):
             at = pl.ds(pl.multiple_of(k * ROWS, ROWS), ROWS)
             here = pl.ds(pl.multiple_of(base + k * ROWS, ROWS), ROWS)
-            goal = targets[here].astype(F32)
-            fmiss = total_of(frefs, at) - goal
-            frozen_loss = 0.5 * jnp.sum(fmiss * fmiss, axis=-1, keepdims=True) / root
-            miss = total_of(lrefs, at) - goal
-            learner_loss = 0.5 * jnp.sum(miss * miss, axis=-1, keepdims=True) / root
-            score = learner_loss - frozen_loss
-            flat_scores[here] = jnp.broadcast_to(score, (ROWS, flat_scores.shape[1]))
-            ograd[here] = (sigmoid(score) * miss / root).astype(BF16)
+            miss = total_of(refs, at) - targets[here].astype(F32)
+            loss = 0.5 * jnp.sum(miss * miss, axis=-1, keepdims=True) / root
+            flat_scores[here] = jnp.broadcast_to(loss, (ROWS, flat_scores.shape[1]))
+            ograd[here] = (miss / root).astype(BF16)
             return carry
 
         lax.fori_loop(0, block // 2 // ROWS, rows, 0)
 
-    fa, fb = frozen.a.stage4(), frozen.b.stage4()
-    la = learner.a.stage4()
-    losses(fa, la, 0)
-    losses(fb, learner.b.stage4(), block // 2)
-    regather = Gather(s, ograd, full, gsend, grecv)
+    def weights(refs, base):
+        def rows(k, carry):
+            at = pl.ds(pl.multiple_of(k * ROWS, ROWS), ROWS)
+            here = pl.ds(pl.multiple_of(base + k * ROWS, ROWS), ROWS)
+            there = pl.ds(pl.multiple_of(s.c * block + base + k * ROWS, ROWS), ROWS)
+            miss = total_of(refs, at) - targets[here].astype(F32)
+            loss = 0.5 * jnp.sum(miss * miss, axis=-1, keepdims=True) / root
+            score = flat_scores[here] - jnp.broadcast_to(loss, (ROWS, flat_scores.shape[1]))
+            flat_scores[here] = score
+            turn_w[there] = sigmoid(score)
+            return carry
+
+        lax.fori_loop(0, block // 2 // ROWS, rows, 0)
+
+    misses(learner.a.stage4(), 0)
+    misses(learner.b.stage4(), block // 2)
+    regather = Gather(s, ograd, again, gsend, grecv)
     regather.start()
+    frozen.ready(3)
+    frozen.a.near_out()
+    frozen.b.stage3()
+    frozen.a.stage3()
+    turn_w[...] = jnp.zeros_like(turn_w)
     outs = []
 
     def emit(src, dst):
         outs.append(pltpu.make_async_copy(src, dst, out_sems.at[len(outs)]))
         outs[-1].start()
 
-    o_scores[...] = flat_scores[...].T[:1]
     gain_acc[...] = jnp.zeros_like(gain_acc)
-    frozen.drain()
 
     learner.drain()
-    summed = GroupSum(s, LATE, fpart, fpaired, ring_l, None, ring_f, fsend, frecv)
+    summed = GroupSum(s, LATE, lpart, lpaired, (nslots, nlast), None, ring_l, lsend, lrecv)
 
     def dp_dev(xx, yy):
         return {"dp": yy * 4 + xx}
@@ -581,7 +592,7 @@
 
         def cols(j, carry):
             at = tile(j, cut)
-            hg = dot_t(rows_of(full, p1, p2), vwd[at, :])
+            hg = dot_t(rows_of(again, p1, p2), vwd[at, :])
             g, u = rows_of(gate, p1, p2, at), rows_of(up, p1, p2, at)
             sigma = sigmoid(g)
             side = hg * sigma
@@ -595,12 +606,40 @@
                 flipped[at, tile(p2, n)] = turned[:, n:]
             return carry
 
-        lax.fori_loop(0, wide, cols, 0)
-
-    for i, events in enumerate(((0, 1, 2, 3), (4, 5), (6, 7), (8,))):
-        regather.arrive(*events)
-        regather.have(i)
-        back(i)
+        lax.fori_loop(0, wide, cols, 0, unroll=True)
+
+    ww = Wires(wsend, wrecv)
+    regather.arrive(0, 1, 2)
+    regather.have(0)
+    back(0)
+    regather.arrive(3, 4)
+    weights(frozen.a.stage4(), 0)
+    weights(frozen.b.stage4(), block // 2)
+    row_w[s.t] = turn_w[...].T[:1]
+    for r in range(1, 16):
+        ww.send(row_w.at[s.t], row_w.at[s.t], r - 1, r - 1, {"tensor": (s.t + r) % 16})
+    regather.arrive(5)
+    regather.have(1)
+    back(1)
+    regather.arrive(6, 7)
+    regather.have(2)
+    back(2)
+    regather.arrive(8)
+    regather.have(3)
+    back(3)
+    o_scores[...] = flat_scores[...].T[:1]
+    for r in range(1, 16):
+        ww.got(row_w.at[(s.t + 16 - r) % 16], r - 1, {"tensor": (s.t + 1) % 16})
+    frozen.drain()
+    columns = jnp.concatenate([row_w[k] for k in range(16)], axis=0).T
+    for p in range(8):
+        both = columns[:, 2 * p : 2 * p + 1] + columns[:, 2 * p + 1 : 2 * p + 2]
+        col_w[p] = jnp.broadcast_to(both, col_w.shape[1:])
+
+    def weigh(ref):
+        for p in range(8):
+            at = pl.ds(p * n, n)
+            ref[:, at] = (ref[:, at].astype(F32) * (row_w[2 * p] + row_w[2 * p + 1])).astype(BF16)
 
     def term(q, lhs, rhs, dd):
         at = tile(dd, cut)
@@ -612,7 +651,7 @@
             term(q, lhs, rhs, row * 4 + ring)
             return code // 8
 
-        lax.fori_loop(lo, hi, one, jnp.int32(order // 8**lo))
+        lax.fori_loop(lo, hi, one, jnp.int32(order // 8**lo), unroll=2)
 
     def normed_part(i):
         p1, p2 = s.pairs(i, LATE)
@@ -620,12 +659,13 @@
         def outs(j, carry):
             at = tile(j, wt)
             value = dot_t(rows_of(gg, p1, p2), vwg[at, :]) + dot_t(rows_of(ug, p1, p2), vwu[at, :])
-            put(fpart, p1, p2, at, value)
+            value = value * jnp.concatenate([col_w[p1, :, :1], col_w[p2, :, :1]], axis=0)
+            put(lpart, p1, p2, at, value)
             gains = value * rows_of(normed, p1, p2, at).astype(F32)
             gain_acc[:, at] += gains.reshape(-1, 8, wt).sum(axis=0)
             return carry
 
-        lax.fori_loop(0, width // wt, outs, 0)
+        lax.fori_loop(0, width // wt, outs, 0, unroll=True)
         summed.pair_send(i)
 
     def ring_start(q, lhs, ring):
@@ -636,10 +676,13 @@
         ring.ready(1, 0)
         ring.ready(3, 1)
 
+    weigh(ggt)
     ring_start(0, ggt, gate_sum)
-    some_terms(2, hid_t, full, DOWN, 0, 4)
+    weigh(hid_t)
+    some_terms(2, hid_t, again, DOWN, 0, 4)
     for off in (2, 1, 3, 0):
         down_sum.ready(off, 1)
+    weigh(ugt)
     ring_start(1, ugt, up_sum)
     normed_part(0)
     normed_part(1)
@@ -658,7 +701,7 @@
     summed.a.stage2()
     summed.b.stage2()
     some_terms(1, ugt, normed, TERMS, 4, 8)
-    some_terms(2, hid_t, full, DOWN, 4, 8)
+    some_terms(2, hid_t, again, DOWN, 4, 8)
     up_sum.stage2()
     down_sum.far_out()
     down_sum.near_out()
@@ -717,7 +760,7 @@
     emit(o_up, out_up)
     finish_plain(o_down, down_sum.stage4())
     emit(o_down, out_down)
-    for wires in (summed, regather.w, gate_sum.w, up_sum.w, down_sum.w, tw, pw):
+    for wires in (summed, regather.w, gate_sum.w, up_sum.w, down_sum.w, tw, pw, ww):
         wires.drain()
     for copy in outs:
         copy.wait()
@@ -775,6 +818,8 @@
         scratch_shapes=[blocks, blocks, vmem((2, 2, block, width), BF16), pre, pre, turned]
         + [vmem((4 * block, hidden), BF16), blocks, blocks]
         + twice((8, block), (6, half), (half,), (4, half), (2, half // 2), (2, half))
+        + [blocks, vmem((6, half, width), BF16), vmem((half, width), BF16)]
+        + [vmem((2 * block, 128), F32), vmem((16, 1, 128), F32), vmem((8, 2 * block, 128), F32)]
         + [vmem((width, hidden), BF16)] * 2
         + [vmem((hidden, width), BF16), vmem((3, 8, hidden, cut), BF16)]
         + [vmem((block, width), BF16), vmem((block, 128), F32), flat, flat, turned, turned]
@@ -782,7 +827,7 @@
         + [vmem((k, hidden // h, cut), BF16) for k, h in ((4, 1), (2, 2), (2, 1))]
         + [vmem((8, width), F32), vmem((16, 1, width), F32), vmem((8, 1, width), F32)]
         + held
-        + dma(6, 6, 25, 25, 25, 25, 25, 25, 14, 14, 10, 10, 15, 15, 7, 7),
+        + dma(6, 6, 25, 25, 25, 25, 25, 25, 14, 14, 10, 10, 15, 15, 7, 7, 15, 15),
         compiler_params=pltpu.CompilerParams(
             has_side_effects=True, vmem_limit_bytes=VMEM_LIMIT, collective_id=1
         ),

time: 140 us -> 133 us (0.950)
  Pallas kernels: 139 us -> 132 us
    pallas_call x1, Pallas kernels: 137 us -> 130 us  [local(): pl.pallas_call(kernel, out_shape=shapes, in_specs=[here] * 4 + [away] * 6...]
where the time goes in v3:
time: 133 us
  Pallas kernels  132 us (99%)
    pallas_call x1, Pallas kernels, local(): pl.pallas_call(kernel, out_shape=shapes, in_specs=[here] * 4 + [away] * 6...  130 us

profile of v3, /device:TPU:1, one launch (start us, length us, event | category | flops | bytes accessed | tf_op | source)
XLA Modules:
  0.0 132.9 jit_solution(15933112558368811401)
XLA Ops:
  0.6 129.7 %step.1 = (f32[1,64]{1,0:T(1,128)}, bf16[64,2048]{1,0:T(8,128)(2,1)}, f32[1,2048]{1,0:T(1,128)}, f32[256,512]{1,0:T(8,128)}, f32[256,512]{1,0:T(8,128)}, /*index=5*/f32[512,256]{1,0:T(8,128)}) custom-call(bf16[64,2048]{1,0:T(8,128)(2,1)} %tokens.1, bf16[64,2048]{1,0:T(8,128)(2,1)} %targets.1, f32[1,2048]{1,0:T(1,128)} %bitcast.4, f32[1,2048]{1,0:T(1,128)} %bitcast.5, ...), custom_call_target="tpu_custom_call" | custom-call | tf_op jit(solution)/shard_map/step/pallas_call | solution.py:813
  130.3 2.4 %hand_over.1 = (f32[1,64]{1,0:T(1,128)}, bf16[64,2048]{1,0:T(8,128)(2,1)}, f32[1,2048]{1,0:T(1,128)}, f32[256,512]{1,0:T(8,128)}, f32[256,512]{1,0:T(8,128)}, /*index=5*/f32[512,256]{1,0:T(8,128)}) custom-call(f32[1,64]{1,0:T(1,128)} %get-tuple-element.18.refs_0_, bf16[64,2048]{1,0:T(8,128)(2,1)} %get-tuple-element.19.refs_1_, ...), custom_call_target="tpu_custom_call" | custom-call | tf_op jit(solution)/shard_map/hand_over/pallas_call | solution.py:839

commit v4 on v3

--- a/solution.py
+++ b/solution.py
@@ -19,42 +19,35 @@
     return sum(p * 8**k for k, p in enumerate(order))
 
 
-ARRIVAL = digits(0, 3, 1, 4, 2, 7, 6, 5)
-LATE = digits(6, 2, 5, 3, 7, 4, 1, 0)
+ARRIVAL = ((0,), (3, 1), (4,), (7, 2), (6, 5))
+LATE = ((6, 2), (5, 3), (7, 4), (1, 0))
 TERMS = digits(2, 6, 5, 3, 1, 7, 0, 4)
 DOWN = digits(2, 1, 3, 0, 6, 5, 7, 4)
 ALL, A, B, A0, A1, B0, B1 = (0, 4), (0, 2), (2, 4), (0, 1), (1, 2), (2, 3), (3, 4)
 
 
 class Wires:
-    def __init__(self, send_sems, recv_sems):
-        self.send_sems, self.recv_sems, self.sent = send_sems, recv_sems, []
-
-    def send(self, src, dst, out, into, device):
-        copy = pltpu.make_async_remote_copy(
+    def __init__(self, send_sem, recv_sems):
+        self.send_sem, self.recv_sems = send_sem, recv_sems
+
+    def copy(self, src, dst, into, device):
+        return pltpu.make_async_remote_copy(
             src_ref=src,
             dst_ref=dst,
-            send_sem=self.send_sems.at[out],
+            send_sem=self.send_sem,
             recv_sem=self.recv_sems.at[into],
             device_id=device,
             device_id_type=MESH,
         )
-        copy.start()
-        self.sent.append(copy)
+
+    def send(self, src, dst, out, into, device):
+        self.copy(src, dst, into, device).start()
 
     def got(self, ref, into, device):
-        pltpu.make_async_remote_copy(
-            src_ref=ref,
-            dst_ref=ref,
-            send_sem=self.send_sems.at[0],
-            recv_sem=self.recv_sems.at[into],
-            device_id=device,
-            device_id_type=MESH,
-        ).wait_recv()
-
-    def drain(self):
-        for copy in self.sent:
-            copy.wait_send()
+        self.copy(ref, ref, into, device).wait_recv()
+
+    def drain(self, ref, device):
+        self.copy(ref, ref, 0, device).wait_send()
 
 
 class Seat:
@@ -68,14 +61,8 @@
     def dev(self, z, y, c):
         return {"tensor": z * 4 + y * 2 + c}
 
-    def pairs_of(self, code):
-        first, second = code % 8, (code // 8) % 8
-        return tuple(
-            ((self.z + p % 4) % 4) * 2 + (self.y + p // 4) % 2 for p in (first, second)
-        )
-
-    def pairs(self, i, order):
-        return self.pairs_of(order // 64**i)
+    def pairs(self, i, chunks):
+        return tuple(((self.z + p % 4) % 4) * 2 + (self.y + p // 4) % 2 for p in chunks[i])
 
 
 def meet(devices):
@@ -164,6 +151,7 @@
             if e == 7:
                 self.got(zm, o, B, 11)
                 self.pass_on(zm, o, ALL, 22, 22, sib)
+            if e == 9:
                 self.got(zp, o, B, 13)
                 self.pass_on(zp, o, ALL, 23, 23, sib)
             if e == 8:
@@ -175,8 +163,8 @@
     def have(self, i):
         s = self.s
         sib = s.dev(s.z, s.y, s.s)
-        for p, k in zip(s.pairs(i, ARRIVAL), ((17, 18), (19, 21), (20, 22), (24, 23))[i]):
-            self.w.got(self.full.at[p, s.s], k, sib)
+        for place, p in zip(ARRIVAL[i], s.pairs(i, ARRIVAL)):
+            self.w.got(self.full.at[p, s.s], (17, 19, 20, 18, 21, 23, 24, 22)[place], sib)
 
 
 def fold(dst, refs):
@@ -297,8 +285,8 @@
 
 
 class GroupSum:
-    def __init__(self, seat, order, partial, paired, ring_a, row_a, ring_b, send_sems, recv_sems):
-        self.s, self.order, self.partial, self.paired = seat, order, partial, paired
+    def __init__(self, seat, chunks, partial, paired, ring_a, row_a, ring_b, send_sems, recv_sems):
+        self.s, self.chunks, self.partial, self.paired = seat, chunks, partial, paired
         self.w = Wires(send_sems, recv_sems)
         half = paired.shape[1] // 2
 
@@ -313,24 +301,22 @@
         self.a = form(block(0), dev, seat.z, seat.y, *buffers, send_sems, recv_sems, 15)
         self.b = RingFirst(block(1), dev, seat.z, seat.y, *ring_b, send_sems, recv_sems, 8)
 
+    def places(self, i):
+        first = sum(len(c) for c in self.chunks[:i])
+        return [(first + j, p) for j, p in enumerate(self.s.pairs(i, self.chunks))]
+
     def pair_send(self, i):
         s = self.s
-        for j, p in enumerate(s.pairs(i, self.order)):
-            k = 2 * i + j
+        for k, p in self.places(i):
             self.w.send(self.partial.at[p, s.s], self.paired.at[p], k, k, s.dev(s.z, s.y, s.s))
 
     def ready(self, i):
         s = self.s
-        for j, p in enumerate(s.pairs(i, self.order)):
-            self.w.got(self.paired.at[p], 2 * i + j, s.dev(s.z, s.y, s.s))
-        for j in range(2):
-            place = self.order // 8 ** (2 * i + j) % 8
+        for k, p in self.places(i):
+            self.w.got(self.paired.at[p], k, s.dev(s.z, s.y, s.s))
+        for place in self.chunks[i]:
             self.b.ready(place % 4, place // 4)
             self.a.ready(place % 4, place // 4)
-
-    def drain(self):
-        for w in (self.w, self.a.w, self.b.w):
-            w.drain()
 
 
 def total_of(refs, at):
@@ -356,8 +342,8 @@
     return pl.ds(pl.multiple_of(j * size, size), size)
 
 
-def rows_of(ref, p1, p2, at=slice(None)):
-    parts = [ref[p, ..., at] for p in (p1, p2)]
+def rows_of(ref, ps, at=slice(None)):
+    parts = [ref[p, ..., at] for p in ps]
     return jnp.concatenate([v.reshape(-1, v.shape[-1]) for v in parts], axis=0)
 
 
@@ -390,20 +376,24 @@
                 moves.append((part, terms.at[q, j * deep + k], q))
     moves += [(fd.at[:, pl.ds(k * cut, cut)], terms.at[2, k], 2) for k in range(8)]
 
+    def load(moves):
+        for src, dst, k in moves:
+            pltpu.make_async_copy(src, dst, load_sems.at[k]).start()
+
     def loaded(ref, k):
         pltpu.make_async_copy(ref, ref, load_sems.at[k]).wait()
 
     peers = [{"tensor": (s.t + r) % 16} for r in range(1, 16)]
     peers += [{"dp": (d + r) % 8} for r in range(1, 8)]
+    load(moves[:3])
     meet(peers)
-    gather = Gather(s, tokens, full, gsend, grecv)
+    gather = Gather(s, tokens, full, gsend.at[0], grecv)
     gather.start()
-    for src, dst, k in moves:
-        pltpu.make_async_copy(src, dst, load_sems.at[k]).start()
+    load(moves[3:])
     ring_l, ring_f = (lslots, llast), (fslots, flast)
     row_l, row_f = (lacross, lfar, lnear), (facross, ffar, fnear)
-    learner = GroupSum(s, ARRIVAL, lpart, lpaired, None, row_l, ring_l, lsend, lrecv)
-    frozen = GroupSum(s, LATE, fpart, fpaired, None, row_f, ring_f, fsend, frecv)
+    learner = GroupSum(s, ARRIVAL, lpart, lpaired, None, row_l, ring_l, lsend.at[0], lrecv)
+    frozen = GroupSum(s, LATE, fpart, fpaired, None, row_f, ring_f, fsend.at[0], frecv)
 
     def unit(ref, at):
         v = ref[at].astype(F32)
@@ -423,14 +413,14 @@
 
             lax.fori_loop(0, 2, one, 0)
 
-    def put(part, p1, p2, cols, value):
-        value = value.astype(BF16).reshape(2, 2, block, value.shape[-1])
-        part[p1, :, :, cols] = value[0]
-        part[p2, :, :, cols] = value[1]
+    def put(part, ps, cols, value):
+        value = value.astype(BF16).reshape(len(ps), 2, block, value.shape[-1])
+        for k, p in enumerate(ps):
+            part[p, :, :, cols] = value[k]
 
     def frozen_hidden():
         def cols(j, carry):
-            lhs = rows_of(fnormed, 0, 1)
+            lhs = rows_of(fnormed, (0, 1))
             at = pl.ds(j * deep, deep)
             g = dot(lhs, terms[0, at].reshape(width, cut))
             u = dot(lhs, terms[1, at].reshape(width, cut))
@@ -440,12 +430,12 @@
         lax.fori_loop(0, wide, cols, 0, unroll=True)
 
     def frozen_out(i):
-        p1, p2 = s.pairs(i, LATE)
+        ps = s.pairs(i, LATE)
 
         def outs(j, carry):
             lhs = hid[...]
             value = jnp.concatenate([dot(lhs, terms[2, 2 * j + k]) for k in range(2)], axis=1)
-            put(fpart, p1, p2, tile(j, wt), value)
+            put(fpart, ps, tile(j, wt), value)
             return carry
 
         lax.fori_loop(0, 4, outs, 0, unroll=True)
@@ -461,70 +451,79 @@
             lax.fori_loop(0, 2, one, 0)
 
     def learner_hidden(i):
-        p1, p2 = s.pairs(i, ARRIVAL)
+        ps = s.pairs(i, ARRIVAL)
 
         def cols(j, carry):
             at = tile(j, cut)
-            lhs = rows_of(normed, p1, p2)
+            lhs = rows_of(normed, ps)
             g, u = dot(lhs, vwg[:, at]), dot(lhs, vwu[:, at])
-            gate[p1, :, at], gate[p2, :, at] = g[:n], g[n:]
-            up[p1, :, at], up[p2, :, at] = u[:n], u[n:]
             h = g * sigmoid(g) * u
-            hid[:, at] = h.astype(BF16)
+            hid[: n * len(ps), at] = h.astype(BF16)
             ht = h.T.astype(BF16)
-            hid_t[at, tile(p1, n)] = ht[:, :n]
-            hid_t[at, tile(p2, n)] = ht[:, n:]
+            for k, p in enumerate(ps):
+                mine = slice(k * n, k * n + n)
+                gate[p, :, at], up[p, :, at] = g[mine], u[mine]
+                hid_t[at, tile(p, n)] = ht[:, mine]
             return carry
 
         lax.fori_loop(0, wide, cols, 0, unroll=True)
 
     def learner_out(i):
-        p1, p2 = s.pairs(i, ARRIVAL)
+        ps = s.pairs(i, ARRIVAL)
 
         def outs(j, carry):
             at = tile(j, wt)
-            put(lpart, p1, p2, at, dot(hid[...], vwd[:, at]))
+            put(lpart, ps, at, dot(hid[: n * len(ps)], vwd[:, at]))
             return carry
 
         lax.fori_loop(0, width // wt, outs, 0, unroll=True)
         learner.pair_send(i)
 
-    arrivals = (((0, 1, 2), (3, 4), (5,)), ((), (6,), (7,)), ((8,), (), ()), ((), (), ()))
-    for i in range(4):
-        gather.arrive(*arrivals[i][0])
+    arrivals = (
+        ((), (), (), ()),
+        ((0, 1, 2), (3, 4), (), (5,)),
+        ((), (7,), (), (6,)),
+        ((), (9,), (8,), ()),
+        ((), (), (), ()),
+    )
+    for i, events in enumerate(arrivals):
+        gather.arrive(*events[0])
         gather.have(i)
         learner_units(i)
-        gather.arrive(*arrivals[i][1])
+        gather.arrive(*events[1])
         if i == 0:
             for k, ref in ((3, vwg), (4, vwu), (5, vwd)):
                 loaded(ref, k)
         if i > 0:
             learner.ready(i - 1)
+        gather.arrive(*events[2])
         learner_hidden(i)
-        gather.arrive(*arrivals[i][2])
+        gather.arrive(*events[3])
         learner_out(i)
     frozen_units(0)
-    learner.ready(3)
-    gather.w.drain()
+    learner.ready(4)
+    most = normed.at[:, :, :, pl.ds(0, width * 15 // 16)]
+    sib = s.dev(s.z, s.y, s.s)
+    gather.w.drain(most, sib)
     for q in range(3):
         loaded(terms.at[q], q)
     frozen_hidden()
     frozen_out(0)
     frozen_units(1)
-    frozen.ready(0)
     frozen_hidden()
     learner.b.stage2()
+    learner.a.far_out()
+    frozen.ready(0)
     frozen_out(1)
     frozen_units(2)
-    learner.a.far_out()
+    learner.a.near_out()
     frozen.ready(1)
     frozen_hidden()
-    learner.a.near_out()
+    learner.b.stage3()
     frozen_out(2)
+    learner.a.stage3()
     frozen_units(3)
-    learner.b.stage3()
     frozen.ready(2)
-    learner.a.stage3()
     frozen.b.stage2()
     frozen_hidden()
     frozen.a.far_out()
@@ -559,7 +558,7 @@
 
     misses(learner.a.stage4(), 0)
     misses(learner.b.stage4(), block // 2)
-    regather = Gather(s, ograd, again, gsend, grecv)
+    regather = Gather(s, ograd, again, gsend.at[0], grecv)
     regather.start()
     frozen.ready(3)
     frozen.a.near_out()
@@ -574,8 +573,8 @@
 
     gain_acc[...] = jnp.zeros_like(gain_acc)
 
-    learner.drain()
-    summed = GroupSum(s, LATE, lpart, lpaired, (nslots, nlast), None, ring_l, lsend, lrecv)
+    learner.w.drain(most, sib)
+    summed = GroupSum(s, LATE, lpart, lpaired, (nslots, nlast), None, ring_l, lsend.at[0], lrecv)
 
     def dp_dev(xx, yy):
         return {"dp": yy * 4 + xx}
@@ -583,35 +582,38 @@
     def dp_block(q):
         return lambda xx, yy: [terms.at[q, yy * 4 + xx]]
 
-    gate_sum = RingFirst(dp_block(0), dp_dev, x, yl, gslots, glast, qsend, qrecv, 0)
-    up_sum = RingFirst(dp_block(1), dp_dev, x, yl, uslots, ulast, qsend, qrecv, 7)
-    down_sum = RowFirst(dp_block(2), dp_dev, x, yl, dslots, dfar, dlast, dsend, drecv, 0)
+    gate_sum = RingFirst(dp_block(0), dp_dev, x, yl, gslots, glast, qsend.at[0], qrecv, 0)
+    up_sum = RingFirst(dp_block(1), dp_dev, x, yl, uslots, ulast, qsend.at[1], qrecv, 7)
+    down_sum = RowFirst(dp_block(2), dp_dev, x, yl, dslots, dfar, dlast, dsend.at[0], drecv, 0)
 
     def back(i):
-        p1, p2 = s.pairs(i, ARRIVAL)
+        ps = s.pairs(i, ARRIVAL)
 
         def cols(j, carry):
             at = tile(j, cut)
-            hg = dot_t(rows_of(again, p1, p2), vwd[at, :])
-            g, u = rows_of(gate, p1, p2, at), rows_of(up, p1, p2, at)
+            hg = dot_t(rows_of(again, ps), vwd[at, :])
+            g, u = rows_of(gate, ps, at), rows_of(up, ps, at)
             sigma = sigmoid(g)
             side = hg * sigma
             ggrad = side * u * (1.0 + g * (1.0 - sigma))
             ugrad = side * g
             for value, plain, flipped in ((ggrad, gg, ggt), (ugrad, ug, ugt)):
-                low = value.astype(BF16)
-                plain[p1, :, at], plain[p2, :, at] = low[:n], low[n:]
-                turned = value.T.astype(BF16)
-                flipped[at, tile(p1, n)] = turned[:, :n]
-                flipped[at, tile(p2, n)] = turned[:, n:]
+                low, turned = value.astype(BF16), value.T.astype(BF16)
+                for k, p in enumerate(ps):
+                    mine = slice(k * n, k * n + n)
+                    plain[p, :, at] = low[mine]
+                    flipped[at, tile(p, n)] = turned[:, mine]
             return carry
 
         lax.fori_loop(0, wide, cols, 0, unroll=True)
 
-    ww = Wires(wsend, wrecv)
-    regather.arrive(0, 1, 2)
+    ww = Wires(wsend.at[0], wrecv)
+    regather.arrive(0, 1)
     regather.have(0)
     back(0)
+    regather.arrive(2)
+    regather.have(1)
+    back(1)
     regather.arrive(3, 4)
     weights(frozen.a.stage4(), 0)
     weights(frozen.b.stage4(), block // 2)
@@ -619,18 +621,18 @@
     for r in range(1, 16):
         ww.send(row_w.at[s.t], row_w.at[s.t], r - 1, r - 1, {"tensor": (s.t + r) % 16})
     regather.arrive(5)
-    regather.have(1)
-    back(1)
-    regather.arrive(6, 7)
     regather.have(2)
     back(2)
-    regather.arrive(8)
+    regather.arrive(7, 6, 9)
     regather.have(3)
     back(3)
+    regather.arrive(8)
+    regather.have(4)
+    back(4)
     o_scores[...] = flat_scores[...].T[:1]
     for r in range(1, 16):
         ww.got(row_w.at[(s.t + 16 - r) % 16], r - 1, {"tensor": (s.t + 1) % 16})
-    frozen.drain()
+    frozen.w.drain(most, sib)
     columns = jnp.concatenate([row_w[k] for k in range(16)], axis=0).T
     for p in range(8):
         both = columns[:, 2 * p : 2 * p + 1] + columns[:, 2 * p + 1 : 2 * p + 2]
@@ -651,17 +653,17 @@
             term(q, lhs, rhs, row * 4 + ring)
             return code // 8
 
-        lax.fori_loop(lo, hi, one, jnp.int32(order // 8**lo), unroll=2)
+        lax.fori_loop(lo, hi, one, jnp.int32(order // 8**lo), unroll=True)
 
     def normed_part(i):
-        p1, p2 = s.pairs(i, LATE)
+        ps = s.pairs(i, LATE)
 
         def outs(j, carry):
             at = tile(j, wt)
-            value = dot_t(rows_of(gg, p1, p2), vwg[at, :]) + dot_t(rows_of(ug, p1, p2), vwu[at, :])
-            value = value * jnp.concatenate([col_w[p1, :, :1], col_w[p2, :, :1]], axis=0)
-            put(lpart, p1, p2, at, value)
-            gains = value * rows_of(normed, p1, p2, at).astype(F32)
+            value = dot_t(rows_of(gg, ps), vwg[at, :]) + dot_t(rows_of(ug, ps), vwu[at, :])
+            value = value * jnp.concatenate([col_w[p, :, :1] for p in ps], axis=0)
+            put(lpart, ps, at, value)
+            gains = value * rows_of(normed, ps, at).astype(F32)
             gain_acc[:, at] += gains.reshape(-1, 8, wt).sum(axis=0)
             return carry
 
@@ -692,7 +694,7 @@
     normed_part(3)
     summed.ready(2)
     gain_t[s.t] = jnp.sum(gain_acc[...], axis=0, keepdims=True) / lgain[...]
-    tw, pw = Wires(tsend, trecv), Wires(psend, precv)
+    tw, pw = Wires(tsend.at[0], trecv), Wires(psend.at[0], precv)
     for r in range(1, 16):
         tw.send(gain_t.at[s.t], gain_t.at[s.t], r - 1, r - 1, {"tensor": (s.t + r) % 16})
     some_terms(0, ggt, normed, TERMS, 4, 8)
@@ -760,8 +762,17 @@
     emit(o_up, out_up)
     finish_plain(o_down, down_sum.stage4())
     emit(o_down, out_down)
-    for wires in (summed, regather.w, gate_sum.w, up_sum.w, down_sum.w, tw, pw, ww):
-        wires.drain()
+    for wires, ref in (
+        (summed.w, most),
+        (regather.w, most),
+        (gate_sum.w, terms.at[0, pl.ds(0, 7)]),
+        (up_sum.w, terms.at[1, pl.ds(0, 7)]),
+        (down_sum.w, terms.at[2, pl.ds(0, 7)]),
+        (tw, gain_t.at[pl.ds(0, 15)]),
+        (pw, gain_d.at[pl.ds(0, 7)]),
+        (ww, row_w.at[pl.ds(0, 15)]),
+    ):
+        wires.drain(ref, sib)
     for copy in outs:
         copy.wait()
 
@@ -827,7 +838,7 @@
         + [vmem((k, hidden // h, cut), BF16) for k, h in ((4, 1), (2, 2), (2, 1))]
         + [vmem((8, width), F32), vmem((16, 1, width), F32), vmem((8, 1, width), F32)]
         + held
-        + dma(6, 6, 25, 25, 25, 25, 25, 25, 14, 14, 10, 10, 15, 15, 7, 7, 15, 15),
+        + dma(6, 6, 1, 25, 1, 25, 1, 25, 2, 14, 1, 10, 1, 15, 1, 7, 1, 15),
         compiler_params=pltpu.CompilerParams(
             has_side_effects=True, vmem_limit_bytes=VMEM_LIMIT, collective_id=1
         ),

time: 133 us -> 128 us (0.962)
  Pallas kernels: 132 us -> 127 us
    pallas_call x1, Pallas kernels: 130 us -> 125 us  [local(): pl.pallas_call(kernel, out_shape=shapes, in_specs=[here] * 4 + [away] * 6...]
where the time goes in v4:
time: 128 us
  Pallas kernels  127 us (99%)
    pallas_call x1, Pallas kernels, local(): pl.pallas_call(kernel, out_shape=shapes, in_specs=[here] * 4 + [away] * 6...  125 us

profile of v4, /device:TPU:1, one launch (start us, length us, event | category | flops | bytes accessed | tf_op | source)
XLA Modules:
  0.0 127.9 jit_solution(3709378987118803731)
XLA Ops:
  0.6 124.7 %step.1 = (f32[1,64]{1,0:T(1,128)}, bf16[64,2048]{1,0:T(8,128)(2,1)}, f32[1,2048]{1,0:T(1,128)}, f32[256,512]{1,0:T(8,128)}, f32[256,512]{1,0:T(8,128)}, /*index=5*/f32[512,256]{1,0:T(8,128)}) custom-call(bf16[64,2048]{1,0:T(8,128)(2,1)} %tokens.1, bf16[64,2048]{1,0:T(8,128)(2,1)} %targets.1, f32[1,2048]{1,0:T(1,128)} %bitcast.4, f32[1,2048]{1,0:T(1,128)} %bitcast.5, ...), custom_call_target="tpu_custom_call" | custom-call | tf_op jit(solution)/shard_map/step/pallas_call | solution.py:824
  125.4 2.4 %hand_over.1 = (f32[1,64]{1,0:T(1,128)}, bf16[64,2048]{1,0:T(8,128)(2,1)}, f32[1,2048]{1,0:T(1,128)}, f32[256,512]{1,0:T(8,128)}, f32[256,512]{1,0:T(8,128)}, /*index=5*/f32[512,256]{1,0:T(8,128)}) custom-call(f32[1,64]{1,0:T(1,128)} %get-tuple-element.18.refs_0_, bf16[64,2048]{1,0:T(8,128)(2,1)} %get-tuple-element.19.refs_1_, ...), custom_call_target="tpu_custom_call" | custom-call | tf_op jit(solution)/shard_map/hand_over/pallas_call | solution.py:850

commit v5 on v4

--- a/solution.py
+++ b/solution.py
@@ -348,11 +348,11 @@
 
 
 def kernel(
-    tokens, targets, lgain, fgain, wg, wu, wd, fg, fu, fd,
+    tokens_in, targets_in, lgain_in, fgain_in, wg, wu, wd, fg, fu, fd,
     scores, grad_tokens, grad_gain, out_gate, out_up, out_down,
     full, normed, fnormed, gate, up, hid_t, hid, lpart, fpart,
     lpaired, fpaired, lslots, fslots, llast, flast, lacross, facross, lfar, ffar, lnear, fnear,
-    again, nslots, nlast, turn_w, row_w, col_w,
+    again, nslots, nlast, turn_w, row_w, col_w, tokens, targets, lgain, fgain,
     vwg, vwu, vwd, terms, ograd, flat_scores,
     gg, ug, ggt, ugt, gslots, glast, uslots, ulast, dslots, dfar, dlast, gain_acc, gain_t, gain_d,
     o_scores, o_tokens, o_gain, o_gate, o_up, o_down,
@@ -368,6 +368,8 @@
     deep, wide = width // hidden, hidden // cut
     n = 2 * block
     wt = 2 * cut
+    small = [(tokens_in, tokens, 6), (lgain_in, lgain, 7), (fgain_in, fgain, 8)]
+    small.append((targets_in, targets, 9))
     moves = [(wg, vwg, 3), (wu, vwu, 4), (wd, vwd, 5)]
     for q, src in ((0, fg), (1, fu)):
         for j in range(wide):
@@ -385,11 +387,16 @@
 
     peers = [{"tensor": (s.t + r) % 16} for r in range(1, 16)]
     peers += [{"dp": (d + r) % 8} for r in range(1, 8)]
+    load(small)
     load(moves[:3])
     meet(peers)
+    loaded(tokens, 6)
     gather = Gather(s, tokens, full, gsend.at[0], grecv)
     gather.start()
     load(moves[3:])
+    loaded(lgain, 7)
+    loaded(fgain, 8)
+    loaded(targets, 9)
     ring_l, ring_f = (lslots, llast), (fslots, flast)
     row_l, row_f = (lacross, lfar, lnear), (facross, ffar, fnear)
     learner = GroupSum(s, ARRIVAL, lpart, lpaired, None, row_l, ring_l, lsend.at[0], lrecv)
@@ -619,7 +626,7 @@
     weights(frozen.b.stage4(), block // 2)
     row_w[s.t] = turn_w[...].T[:1]
     for r in range(1, 16):
-        ww.send(row_w.at[s.t], row_w.at[s.t], r - 1, r - 1, {"tensor": (s.t + r) % 16})
+        ww.send(row_w.at[s.t], row_w.at[s.t], 0, 0, {"tensor": (s.t + r) % 16})
     regather.arrive(5)
     regather.have(2)
     back(2)
@@ -629,15 +636,7 @@
     regather.arrive(8)
     regather.have(4)
     back(4)
-    o_scores[...] = flat_scores[...].T[:1]
-    for r in range(1, 16):
-        ww.got(row_w.at[(s.t + 16 - r) % 16], r - 1, {"tensor": (s.t + 1) % 16})
-    frozen.w.drain(most, sib)
-    columns = jnp.concatenate([row_w[k] for k in range(16)], axis=0).T
-    for p in range(8):
-        both = columns[:, 2 * p : 2 * p + 1] + columns[:, 2 * p + 1 : 2 * p + 2]
-        col_w[p] = jnp.broadcast_to(both, col_w.shape[1:])
-
+    ww.got(row_w.at[pl.ds(0, 15)], 0, sib)
     def weigh(ref):
         for p in range(8):
             at = pl.ds(p * n, n)
@@ -686,6 +685,12 @@
         down_sum.ready(off, 1)
     weigh(ugt)
     ring_start(1, ugt, up_sum)
+    frozen.w.drain(most, sib)
+    o_scores[...] = flat_scores[...].T[:1]
+    columns = jnp.concatenate([row_w[k] for k in range(16)], axis=0).T
+    for p in range(8):
+        both = columns[:, 2 * p : 2 * p + 1] + columns[:, 2 * p + 1 : 2 * p + 2]
+        col_w[p] = jnp.broadcast_to(both, col_w.shape[1:])
     normed_part(0)
     normed_part(1)
     summed.ready(0)
@@ -696,7 +701,7 @@
     gain_t[s.t] = jnp.sum(gain_acc[...], axis=0, keepdims=True) / lgain[...]
     tw, pw = Wires(tsend.at[0], trecv), Wires(psend.at[0], precv)
     for r in range(1, 16):
-        tw.send(gain_t.at[s.t], gain_t.at[s.t], r - 1, r - 1, {"tensor": (s.t + r) % 16})
+        tw.send(gain_t.at[s.t], gain_t.at[s.t], 0, 0, {"tensor": (s.t + r) % 16})
     some_terms(0, ggt, normed, TERMS, 4, 8)
     gate_sum.stage2()
     summed.ready(3)
@@ -709,11 +714,10 @@
     down_sum.near_out()
     summed.a.stage3()
     summed.b.stage3()
-    for r in range(1, 16):
-        tw.got(gain_t.at[(s.t + 16 - r) % 16], r - 1, {"tensor": (s.t + 1) % 16})
+    tw.got(gain_t.at[pl.ds(0, 15)], 0, sib)
     gain_d[d] = jnp.sum(gain_t[...], axis=0)
     for r in range(1, 8):
-        pw.send(gain_d.at[d], gain_d.at[d], r - 1, r - 1, {"dp": (d + r) % 8})
+        pw.send(gain_d.at[d], gain_d.at[d], 0, 0, {"dp": (d + r) % 8})
     gate_sum.stage3()
     up_sum.stage3()
     down_sum.stage3()
@@ -734,8 +738,7 @@
     token_grads(summed.a.stage4(), 0)
     token_grads(summed.b.stage4(), block // 2)
     emit(o_tokens, grad_tokens)
-    for r in range(1, 8):
-        pw.got(gain_d.at[(d + 8 - r) % 8], r - 1, {"dp": (d + 1) % 8})
+    pw.got(gain_d.at[pl.ds(0, 7)], 0, sib)
     o_gain[...] = jnp.sum(gain_d[...], axis=0)
     emit(o_gain, grad_gain)
     emit(o_scores, scores)
@@ -797,7 +800,6 @@
     block, width = tokens.shape
     hidden = learner_gate.shape[1]
     cut, group, half = width // 8, 16 * block, block // 2
-    here = pl.BlockSpec(memory_space=pltpu.VMEM)
     away = pl.BlockSpec(memory_space=pl.ANY)
     shape, vmem = jax.ShapeDtypeStruct, pltpu.VMEM
 
@@ -824,13 +826,15 @@
     results = pl.pallas_call(
         kernel,
         out_shape=shapes,
-        in_specs=[here] * 4 + [away] * 6,
+        in_specs=[away] * 10,
         out_specs=[away] * 6,
         scratch_shapes=[blocks, blocks, vmem((2, 2, block, width), BF16), pre, pre, turned]
         + [vmem((4 * block, hidden), BF16), blocks, blocks]
         + twice((8, block), (6, half), (half,), (4, half), (2, half // 2), (2, half))
         + [blocks, vmem((6, half, width), BF16), vmem((half, width), BF16)]
         + [vmem((2 * block, 128), F32), vmem((16, 1, 128), F32), vmem((8, 2 * block, 128), F32)]
+        + [vmem((block, width), BF16)] * 2
+        + [vmem((1, width), F32)] * 2
         + [vmem((width, hidden), BF16)] * 2
         + [vmem((hidden, width), BF16), vmem((3, 8, hidden, cut), BF16)]
         + [vmem((block, width), BF16), vmem((block, 128), F32), flat, flat, turned, turned]
@@ -838,7 +842,7 @@
         + [vmem((k, hidden // h, cut), BF16) for k, h in ((4, 1), (2, 2), (2, 1))]
         + [vmem((8, width), F32), vmem((16, 1, width), F32), vmem((8, 1, width), F32)]
         + held
-        + dma(6, 6, 1, 25, 1, 25, 1, 25, 2, 14, 1, 10, 1, 15, 1, 7, 1, 15),
+        + dma(10, 6, 1, 25, 1, 25, 1, 25, 2, 14, 1, 10, 1, 1, 1, 1, 1, 1),
         compiler_params=pltpu.CompilerParams(
             has_side_effects=True, vmem_limit_bytes=VMEM_LIMIT, collective_id=1
         ),

time: 128 us -> 127 us (level)
    pallas_call x1, Pallas kernels: 125 us -> 123 us  [local(): pl.pallas_call(kernel, out_shape=shapes, in_specs=[away] * 10, out_specs=...]
where the time goes in v5:
time: 127 us
  Pallas kernels  126 us (99%)
    pallas_call x1, Pallas kernels, local(): pl.pallas_call(kernel, out_shape=shapes, in_specs=[away] * 10, out_specs=...  123 us

profile of v5, /device:TPU:1, one launch (start us, length us, event | category | flops | bytes accessed | tf_op | source)
XLA Modules:
  0.0 126.6 jit_solution(7833850141013957197)
XLA Ops:
  0.6 123.4 %step.1 = (f32[1,64]{1,0:T(1,128)}, bf16[64,2048]{1,0:T(8,128)(2,1)}, f32[1,2048]{1,0:T(1,128)}, f32[256,512]{1,0:T(8,128)}, f32[256,512]{1,0:T(8,128)}, /*index=5*/f32[512,256]{1,0:T(8,128)}) custom-call(bf16[64,2048]{1,0:T(8,128)(2,1)} %tokens_in.1, bf16[64,2048]{1,0:T(8,128)(2,1)} %targets_in.1, f32[1,2048]{1,0:T(1,128)} %bitcast.4, f32[1,2048]{1,0:T(1,128)} %bitcast.5, ...), custom_call_target="tpu_custom_call" | custom-call | tf_op jit(solution)/shard_map/step/pallas_call | solution.py:826
  124.1 2.4 %hand_over.1 = (f32[1,64]{1,0:T(1,128)}, bf16[64,2048]{1,0:T(8,128)(2,1)}, f32[1,2048]{1,0:T(1,128)}, f32[256,512]{1,0:T(8,128)}, f32[256,512]{1,0:T(8,128)}, /*index=5*/f32[512,256]{1,0:T(8,128)}) custom-call(f32[1,64]{1,0:T(1,128)} %get-tuple-element.18.refs_0_, bf16[64,2048]{1,0:T(8,128)(2,1)} %get-tuple-element.19.refs_1_, ...), custom_call_target="tpu_custom_call" | custom-call | tf_op jit(solution)/shard_map/hand_over/pallas_call | solution.py:854
